TPU v7x, 128 devices: a whole 4x4x4 slice. The times are simulated.
128 devices in a mesh: expert: 64 (over y, x, z), etp: 2 (over core).
Axes of the slice: x: 4, y: 4, z: 4, core: 2. Of those that a mesh axis runs over, the one named last changes fastest.
Arguments:
- grad_out: bfloat16 [8192, 3584], P('expert', 'etp'), may hold values from -6 to 6
- combine: bfloat16 [8192, 8], P('expert'), may hold values from 0.099609375 to 2.5
- expert_ids: int32 [8192, 8], P('expert'), may hold values from 0 to 127, all different within a row; in each aligned block of 128 rows (0 to 127, 128 to 255, ...) at most 16 rows name the same one
- saved_gate: bfloat16 [1024, 128, 1024], P(None, 'expert', 'etp'), may hold values from -6 to 6
- saved_up: bfloat16 [1024, 128, 1024], P(None, 'expert', 'etp'), may hold values from -1.5 to 1.5
- gate_weight: bfloat16 [128, 3584, 1024], P('expert', None, 'etp'), may hold values from -0.09375 to 0.09375
- up_weight: bfloat16 [128, 3584, 1024], P('expert', None, 'etp'), may hold values from -0.09375 to 0.09375
- down_weight: bfloat16 [128, 1024, 3584], P('expert', 'etp'), may hold values from -0.09375 to 0.09375
Outputs:
- grad_tokens: bfloat16 [8192, 3584], P('expert', 'etp')
- grad_combine: bfloat16 [8192, 8], P('expert')
Inputs may be any that keep to these rules, and one draw needn't show every extreme that they name: `expert_ids`: each token names 8 different experts. Among the 128 tokens of one block (one index of expert), at most 16 name any one expert, and some blocks reach that bound.
All inputs are finite; a program needn't handle non-finite values.
Results may differ from a plain program's by a relative error of at most 0.012.
Values may be sent and summed in bfloat16 or wider, within the bound.
A program may use at most 192 MiB of HBM per device.

v0:
```python
import jax
import jax.numpy as jnp
from jax import lax
from jax.sharding import PartitionSpec as P


def copy_for_each(x, axis):
    copies = jnp.broadcast_to(x, (lax.axis_size(axis), *x.shape))
    return lax.all_to_all(copies, axis, split_axis=0, concat_axis=0, tiled=True)


def of_everyone(x, axis):
    return copy_for_each(x, axis).astype(jnp.float32).sum(axis=0)


def slot_layout(expert_ids, groups, per_group, capacity):
    token_count, top_count = expert_ids.shape
    experts = groups * per_group
    matches = expert_ids[:, :, None] == jnp.arange(experts, dtype=jnp.int32)[None, None, :]
    expert_loads = jnp.sum(matches.astype(jnp.int32), axis=1)
    earlier = jnp.cumsum(expert_loads, axis=0) - expert_loads
    position = jnp.sum(jnp.where(matches, earlier[:, None, :], 0), axis=2)
    target = expert_ids // per_group
    local_slot = expert_ids % per_group
    flat_slot = (target * capacity + position) * per_group + local_slot
    slot_total = groups * capacity * per_group
    slot_owner = jnp.full((slot_total,), token_count * top_count, jnp.int32)
    slot_owner = slot_owner.at[flat_slot.reshape(-1)].set(
        jnp.arange(token_count * top_count, dtype=jnp.int32)
    )
    return (flat_slot, slot_owner)


def on_device(
    grad_out, combine, expert_ids, saved_gate, saved_up, gate_weight, up_weight, down_weight
):
    groups = lax.axis_size("expert")
    per_group = gate_weight.shape[0]
    half_width = grad_out.shape[1]
    token_count, top_count = expert_ids.shape
    capacity = saved_gate.shape[0] // groups
    slot_rows_count = groups * capacity
    flat_slot, slot_owner = slot_layout(expert_ids, groups, per_group, capacity)
    source_token = slot_owner // top_count
    weight_flat = jnp.concatenate([combine.reshape(-1), jnp.zeros((1,), jnp.bfloat16)])
    slot_weight = jnp.take(weight_flat, slot_owner, axis=0).reshape(groups, capacity, per_group)
    padded = jnp.concatenate([grad_out, jnp.zeros((1, half_width), jnp.bfloat16)], axis=0)
    outgoing = jnp.take(padded, source_token, axis=0).reshape(
        groups, capacity, per_group, half_width
    )
    arrived, arrived_weight = (
        lax.all_to_all(outgoing, "expert", split_axis=0, concat_axis=0, tiled=True),
        lax.all_to_all(slot_weight, "expert", split_axis=0, concat_axis=0, tiled=True),
    )
    slot_rows = lax.all_gather(
        arrived.reshape(slot_rows_count, per_group, half_width), "etp", axis=2, tiled=True
    )
    grad_hidden = jnp.einsum(
        "rld,lfd->rlf", slot_rows, down_weight, preferred_element_type=jnp.float32
    )
    gate_value = saved_gate.astype(jnp.float32)
    up_value = saved_up.astype(jnp.float32)
    gate_sigmoid = jax.nn.sigmoid(gate_value)
    activated = gate_value * gate_sigmoid
    weight_part = jnp.sum(grad_hidden * activated * up_value, axis=2)
    scaled = arrived_weight.reshape(slot_rows_count, per_group, 1).astype(jnp.float32) * grad_hidden
    grad_gate = (
        scaled * up_value * gate_sigmoid * (1.0 + gate_value * (1.0 - gate_sigmoid))
    ).astype(jnp.bfloat16)
    grad_up = (scaled * activated).astype(jnp.bfloat16)
    partial_value = jnp.einsum(
        "rlf,ldf->rld", grad_gate, gate_weight, preferred_element_type=jnp.float32
    )
    partial_value = partial_value + jnp.einsum(
        "rlf,ldf->rld", grad_up, up_weight, preferred_element_type=jnp.float32
    )
    slot_grad = lax.psum_scatter(
        partial_value.astype(jnp.bfloat16), "etp", scatter_dimension=2, tiled=True
    ).astype(jnp.float32)
    weight_sum = of_everyone(weight_part.astype(jnp.bfloat16), "etp").astype(jnp.float32)
    slot_grad = slot_grad.astype(jnp.bfloat16).reshape(groups, capacity, per_group, half_width)
    slot_dw = weight_sum.astype(jnp.bfloat16).reshape(groups, capacity, per_group)
    returned, returned_weight = (
        lax.all_to_all(slot_grad, "expert", split_axis=0, concat_axis=0, tiled=True),
        lax.all_to_all(slot_dw, "expert", split_axis=0, concat_axis=0, tiled=True),
    )
    gathered = jnp.take(returned.reshape(-1, half_width), flat_slot, axis=0)
    grad_tokens = jnp.sum(gathered.astype(jnp.float32), axis=1).astype(jnp.bfloat16)
    grad_combine = jnp.take(returned_weight.reshape(-1), flat_slot, axis=0)
    return (grad_tokens, grad_combine)


def solution(mesh):
    in_specs = (
        P("expert", "etp"),
        P("expert", None),
        P("expert", None),
        P(None, "expert", "etp"),
        P(None, "expert", "etp"),
        P("expert", None, "etp"),
        P("expert", None, "etp"),
        P("expert", "etp", None),
    )
    out_specs = (P("expert", "etp"), P("expert", None))
    return jax.shard_map(
        on_device, mesh=mesh, in_specs=in_specs, out_specs=out_specs, check_vma=False
    )
```

profile of v0, /device:TPU:34, one launch (start us, length us, event | category | flops | bytes accessed | tf_op | source)
XLA Modules:
  0.0 432.2 jit_solution(15667458970925996139)
XLA Ops:
  7.2 0.8 copy.92
  8.0 0.2 convert_reduce_fusion
  8.2 0.2 reduce_window_sum.11
  8.4 2.4 select_reduce_fusion
  10.9 0.1 reshape.100
  11.0 4.3 scatter_custom_fusion
  15.4 0.5 broadcast_in_dim.69
  15.9 0.5 copy.101
  16.4 1.1 concatenate.7
  17.5 10.6 %gather_fusion.1 = bf16[2048,1792]{1,0:T(8,128)(2,1)} fusion(bf16[129,1792]{1,0:T(8,128)(2,1)S(1)} %concatenate.7, s32[2048]{0:T(1024)S(1)} %get-tuple-element.17), kind=kCustom, calls=%fused_computation.1 | custom fusion | bytes 14688256 | tf_op jit(solution)/shard_map/jit(_take)/gather | solution.py:48
  28.1 15.0 %gather.20 = bf16[64,16,2,1792]{3,2,1,0:T(2,128)(2,1)} reshape(bf16[2048,1792]{1,0:T(8,128)(2,1)} %gather_fusion.1) | data formatting | bytes 14680064 | tf_op jit(solution)/shard_map/jit(_take)/gather | solution.py:48
  43.1 4.8 %copy_select_fusion = bf16[64,16,2,1792]{3,1,2,0:T(8,128)(2,1)S(1)} fusion(bf16[64,16,2,1792]{3,2,1,0:T(2,128)(2,1)} %gather.20, pred[64,16,2]{1,2,0:T(4,128)(4,1)S(1)} %copy.101), kind=kLoop, calls=%fused_computation.7 | loop fusion | flops 3670016 | bytes 14682112 | tf_op jit(solution)/shard_map/jit(_take)/select_n | solution.py:48
  47.9 95.6 %all_to_all.25 = bf16[64,16,2,1792]{3,1,2,0:T(8,128)(2,1)S(1)} all-to-all(bf16[64,16,2,1792]{3,1,2,0:T(8,128)(2,1)S(1)} %copy_select_fusion), channel_id=1, replica_groups=mesh['expert'=64,'etp'=2] {'expert'}, dimensions={0} | all-to-all | bytes 14680064 | tf_op jit(solution)/shard_map/all_to_all | solution.py:52
  143.5 3.5 copy.103
  147.0 0.7 copy-done.2
  147.7 0.1 copy.97
  147.8 0.1 reshape.101
  147.9 13.1 %gather_fusion = bf16[2048]{0:T(1024)(128)(2,1)S(1)} fusion(bf16[1025]{0:T(1024)(128)(2,1)S(1)} %pad_maximum_fusion, s32[2048]{0:T(1024)S(1)} %get-tuple-element.16), kind=kCustom, calls=%fused_computation | custom fusion | bytes 16384 | tf_op jit(solution)/shard_map/jit(_take)/gather | solution.py:46
  161.0 0.5 select_n.73
  161.6 1.1 copy.98
  162.7 6.5 %all-to-all-start = ((bf16[64,16,2]{1,2,0:T(2,128)(2,1)}), bf16[64,16,2]{1,2,0:T(2,128)(2,1)S(1)}, u32[]{:S(2)}, u32[]{:S(2)}) async-start(bf16[64,16,2]{1,2,0:T(2,128)(2,1)} %copy.98), calls=%async_computation | async-start | bytes 65536 | tf_op jit(solution)/shard_map/all_to_all | solution.py:53
  169.2 0.2 reduce-scatter.2.cloned.1.call-start
  169.4 4.7 %copy.105 = bf16[1024,2,512]{0,2,1:T(8,128)(2,1)} copy(bf16[1024,2,512]{2,1,0:T(2,128)(2,1)S(1)} %copy-done) | data formatting | bytes 4194304 | tf_op args[3]
  174.2 6.3 %copy.104 = bf16[1024,2,512]{0,2,1:T(8,128)(2,1)} copy(bf16[1024,2,512]{2,1,0:T(2,128)(2,1)} %param.12) | data formatting | bytes 4194304 | tf_op args[4]
  180.5 0.1 copy.99
  180.6 0.1 copy.100
  180.7 0.1 reshape.107
  180.8 15.4 %fusion.4 = (bf16[1024,2]{0,1:T(2,128)(2,1)S(1)}, f32[2,1024,512]{1,2,0:T(8,128)}) fusion(bf16[1024,2,512]{0,2,1:T(8,128)(2,1)} %copy.104, bf16[1024,2,512]{0,2,1:T(8,128)(2,1)S(1)} %copy-done.1, bf16[1024,2,3584]{2,0,1:T(8,128)(2,1)} %all-gather.2.cloned.1.call-done, bf16[2,512,3584]{2,1,0:T(8,128)(2,1)} %param.15), kind=kOutput, calls=%fused_computation.16 | convolution fusion | flops 7525627904 | bytes 30412800 | tf_op jit(solution)/shard_map/rld,lfd->rlf/dot_general | solution.py:58
  196.2 18.9 %fusion.10 = f32[2,1024,3584]{2,1,0:T(8,128)} fusion(bf16[2,3584,512]{2,1,0:T(8,128)(2,1)} %param.13, bf16[1024,2,512]{0,2,1:T(8,128)(2,1)} %copy.104, bf16[1024,2,512]{0,2,1:T(8,128)(2,1)S(1)} %copy-done.1, f32[2,1024,512]{1,2,0:T(8,128)} %get-tuple-element.19, f32[1024,2]{0,1:T(2,128)S(1)} %reshape.107), kind=kOutput, calls=%fused_computation.26 | convolution fusion | flops 7529824256 | bytes 45096960 | tf_op jit(solution)/shard_map/rlf,ldf->rld/dot_general | solution.py:71
  215.1 20.6 %fusion = bf16[1024,2,3584]{2,0,1:T(8,128)(2,1)} fusion(f32[2,1024,3584]{2,1,0:T(8,128)} %fusion.10, bf16[2,3584,512]{2,1,0:T(8,128)(2,1)} %param.14, f32[2,1024,512]{1,2,0:T(8,128)} %get-tuple-element.19, f32[1024,2]{0,1:T(2,128)S(1)} %reshape.107, bf16[1024,2,512]{0,2,1:T(8,128)(2,1)S(1)} %copy-done.1), kind=kOutput, calls=%fused_computation.6 | convolution fusion | flops 7539261440 | bytes 57679872 | tf_op jit(solution)/shard_map/rlf,ldf->rld/dot_general | solution.py:74
  235.7 3.7 all_to_all.26
  239.5 0.1 reshape.105
  239.6 0.7 copy.110
  240.2 10.3 %all-to-all-start.4 = ((bf16[64,16,2]{1,2,0:T(2,128)(2,1)}), bf16[64,16,2]{1,2,0:T(2,128)(2,1)S(1)}, u32[]{:S(2)}, u32[]{:S(2)}) async-start(bf16[64,16,2]{1,2,0:T(2,128)(2,1)} %copy.110), calls=%async_computation.5 | async-start | bytes 65536 | tf_op jit(solution)/shard_map/all_to_all | solution.py:85
  250.6 10.4 %reduce-scatter.2.cloned.1.call-done = bf16[1024,2,1792]{2,0,1:T(8,128)(2,1)} async-done(((bf16[1024,2,3584]{2,0,1:T(8,128)(2,1)}), bf16[1024,2,1792]{2,0,1:T(8,128)(2,1)}) %reduce-scatter.2.cloned.1.call-update) | async-done | bytes 7340048 | tf_op jit(solution)/shard_map/reduce_scatter | solution.py:77
  261.0 7.2 %copy.108 = bf16[64,16,2,1792]{3,1,2,0:T(8,128)(2,1)} copy(bf16[64,16,2,1792]{3,1,0,2:T(8,128)(2,1)} %bitcast.30) | data formatting | bytes 14680064 | tf_op jit(solution)/shard_map/reshape | solution.py:81
  268.2 10.5 %all-to-all-start.2 = ((bf16[64,16,2,1792]{3,1,2,0:T(8,128)(2,1)}), bf16[64,16,2,1792]{3,1,2,0:T(8,128)(2,1)}, u32[]{:S(2)}, u32[]{:S(2)}) async-start(bf16[64,16,2,1792]{3,1,2,0:T(8,128)(2,1)} %copy.108), calls=%async_computation.3 | async-start | bytes 14680064 | tf_op jit(solution)/shard_map/all_to_all | solution.py:84
  278.7 0.1 reshape.126
  278.8 0.5 copy.111
  279.3 0.3 reshape.106
  279.6 6.8 %gather_fusion.3 = bf16[1024]{0:T(1024)(128)(2,1)S(1)} fusion(bf16[2048]{0:T(1024)(128)(2,1)S(1)} %reshape.106, s32[1024]{0:T(1024)S(1)} %broadcast_clamp_fusion.1), kind=kCustom, calls=%fused_computation.3 | custom fusion | bytes 8192 | tf_op jit(solution)/shard_map/jit(_take)/gather | solution.py:89
  286.4 0.1 reshape.133
  286.5 0.7 copy.112
  287.2 94.1 %all-to-all-done.2 = bf16[64,16,2,1792]{3,1,2,0:T(8,128)(2,1)} async-done(((bf16[64,16,2,1792]{3,1,2,0:T(8,128)(2,1)}), bf16[64,16,2,1792]{3,1,2,0:T(8,128)(2,1)}, u32[]{:S(2)}, u32[]{:S(2)}) %all-to-all-start.2) | async-done | bytes 7340064 | tf_op jit(solution)/shard_map/all_to_all | solution.py:84
  381.3 11.7 %copy.109 = bf16[64,16,2,1792]{3,2,1,0:T(2,128)(2,1)} copy(bf16[64,16,2,1792]{3,1,2,0:T(8,128)(2,1)} %all-to-all-done.2) | data formatting | bytes 14680064 | tf_op jit(solution)/shard_map/all_to_all | solution.py:84
  393.1 15.6 %reshape.104 = bf16[2048,1792]{1,0:T(8,128)(2,1)} reshape(bf16[64,16,2,1792]{3,2,1,0:T(2,128)(2,1)} %copy.109) | data formatting | bytes 14680064 | tf_op jit(solution)/shard_map/reshape | solution.py:87
  408.6 12.0 %gather_fusion.2 = bf16[1024,1792]{1,0:T(8,128)(2,1)} fusion(bf16[2048,1792]{1,0:T(8,128)(2,1)} %reshape.104, s32[1024]{0:T(1024)S(1)} %broadcast_clamp_fusion.1), kind=kCustom, calls=%fused_computation.2 | custom fusion | bytes 7344128 | tf_op jit(solution)/shard_map/jit(_take)/gather | solution.py:87
  420.6 4.7 %fusion.9 = bf16[128,1792]{1,0:T(8,128)(2,1)} fusion(bf16[1024,1792]{1,0:T(8,128)(2,1)} %gather_fusion.2, pred[128,8]{1,0:T(8,128)(4,1)S(1)} %get-tuple-element.13), kind=kLoop, calls=%fused_computation.25 | loop fusion | flops 3440640 | bytes 4129792 | tf_op jit(solution)/shard_map/reduce_sum | solution.py:88
  (23 shorter events, 0.3 us)
Async XLA Ops:
  7.2 173.6 %all-gather.2.cloned.1.call-start = ((), (), s32[]{:S(2)}) async-start(), calls=%async_computation.6 | async-start | bytes 22020096 | tf_op jit(solution)/shard_map/all_gather | solution.py:55
  147.0 0.7 copy-start.2
  147.7 21.7 %copy-start = (bf16[1024,2,512]{2,1,0:T(2,128)(2,1)S(1)}, bf16[1024,2,512]{2,1,0:T(2,128)(2,1)}, u32[]{:S(2)}) copy-start(bf16[1024,2,512]{2,1,0:T(2,128)(2,1)} %param.11) | copy-start | bytes 6291460
  162.7 17.8 %all-to-all-start = ((bf16[64,16,2]{1,2,0:T(2,128)(2,1)}), bf16[64,16,2]{1,2,0:T(2,128)(2,1)S(1)}, u32[]{:S(2)}, u32[]{:S(2)}) async-start(bf16[64,16,2]{1,2,0:T(2,128)(2,1)} %copy.98), calls=%async_computation | async-start | bytes 65536 | tf_op jit(solution)/shard_map/all_to_all | solution.py:53
  169.2 91.8 %reduce-scatter.2.cloned.1.call-start = ((), (), s32[]{:S(2)}) async-start(), calls=%async_computation.7 | async-start | bytes 22020096 | tf_op jit(solution)/shard_map/reduce_scatter | solution.py:77
  174.2 6.6 %copy-start.1 = (bf16[1024,2,512]{0,2,1:T(8,128)(2,1)S(1)}, bf16[1024,2,512]{0,2,1:T(8,128)(2,1)}, u32[]{:S(2)}) copy-start(bf16[1024,2,512]{0,2,1:T(8,128)(2,1)} %copy.105) | copy-start | bytes 6291460
  240.2 28.0 %all-to-all-start.4 = ((bf16[64,16,2]{1,2,0:T(2,128)(2,1)}), bf16[64,16,2]{1,2,0:T(2,128)(2,1)S(1)}, u32[]{:S(2)}, u32[]{:S(2)}) async-start(bf16[64,16,2]{1,2,0:T(2,128)(2,1)} %copy.110), calls=%async_computation.5 | async-start | bytes 65536 | tf_op jit(solution)/shard_map/all_to_all | solution.py:85
  268.2 113.1 %all-to-all-start.2 = ((bf16[64,16,2,1792]{3,1,2,0:T(8,128)(2,1)}), bf16[64,16,2,1792]{3,1,2,0:T(8,128)(2,1)}, u32[]{:S(2)}, u32[]{:S(2)}) async-start(bf16[64,16,2,1792]{3,1,2,0:T(8,128)(2,1)} %copy.108), calls=%async_computation.3 | async-start | bytes 14680064 | tf_op jit(solution)/shard_map/all_to_all | solution.py:84
Sparse Core Ops, SparseCore 0:
  147.2 27.2 all-gather.1
  235.8 25.0 reduce-scatter.1
where the time goes:
time: 434 us; the launch traced here: 432 us
  local copies, waits for them, and re-layouts  119 us (27%)
  waiting for transfers between devices  105 us (24%)
  blocking collectives  99.3 us (23%)
  matrix products  54.9 us (13%)
  starting transfers between devices  27.6 us (6%)
  between operations  14.2 us (3%)
  other arithmetic  12.5 us (3%)
    all_to_all x1, blocking collectives, on_device(): lax.all_to_all(outgoing, 'expert', split_axis=0, concat_axis=0, tiled=True)  95.6 us
    all_to_all x1, waiting for transfers between devices, on_device(): lax.all_to_all(slot_grad, 'expert', split_axis=0, concat_axis=0, tiled=True)  94.1 us
    gather x2, local copies, waits for them, and re-layouts, on_device(): jnp.take(padded, source_token, axis=0)  25.7 us
    dot_general x1, matrix products, on_device(): jnp.einsum('rlf,ldf->rld', grad_up, up_weight, preferred_element_type=jnp...  20.6 us
    dot_general x1, matrix products, on_device(): jnp.einsum('rlf,ldf->rld', grad_gate, gate_weight, preferred_element_type...  18.9 us
    reshape x1, local copies, waits for them, and re-layouts, on_device(): gathered = jnp.take(returned.reshape(-1, half_width), flat_slot, axis=0)  15.6 us
    dot_general x1, matrix products, on_device(): jnp.einsum('rld,lfd->rlf', slot_rows, down_weight, preferred_element_type...  15.4 us
    unnamed x11, local copies, waits for them, and re-layouts  13.3 us
  transfers between devices with their start and end apart: 5, of which 2 were waited for; matrix products, arithmetic and copies ran while one was open for 10% of the time, Pallas kernels for 0%

commit v1 on v0

v1 whole, which is shorter than its diff:
```python
import functools
import itertools

import jax
import jax.numpy as jnp
from jax import lax
from jax.experimental import pallas as pl
from jax.experimental.pallas import tpu as pltpu
from jax.sharding import PartitionSpec as P

MESH = pl.DeviceIdType.MESH
BF16, F32, I32 = jnp.bfloat16, jnp.float32, jnp.int32
NT = (((1,), (1,)), ((), ()))
TN = (((0,), (0,)), ((), ()))
CAP = 16
AXES = ((0, 1, 2), (1, 2, 0), (2, 0, 1))


class Plan:
    def __init__(self, n, half, ff, top, tiles, step):
        self.n, self.half, self.ff, self.top, self.step = n, half, ff, top, step
        self.part = (half + 128) // 3
        self.wide = 3 * self.part
        self.widths = (self.part, self.part, self.part - 128)
        self.order = sorted(itertools.product(range(n), repeat=3), key=lambda d: (max(d), d))
        self.slot = {d: i for i, d in enumerate(self.order)}
        self.tiles, start = [], 0
        for count in tiles:
            self.tiles.append((start, count))
            start += count
        self.most = max(tiles)
        self.planes = n * n
        self.peers = [d for d in self.order if 0 < sum(v > 0 for v in d) < 3]

    def along(self, f, values):
        out = [0, 0, 0]
        for axis, value in zip(AXES[f], values):
            out[axis] = value
        return tuple(out)

    def seen(self, f, d):
        return tuple(d[axis] for axis in AXES[f])


def kernel(p, ids_ref, cw_ref, go_ref, sg_ref, su_ref, gw_ref, uw_ref, dn_ref, gt_ref, gc_ref,
           xo, xp, uin, s0, s1, s2, r0, r1, r2, g0, g1, g2, gm, ts, tr, gcs, gcr, codes, cws, meta,
           dno, dnp, gwo, gwp, uwo, uwp, sgt, sut, gbuf, ggb, gub,
           wsem, s1s, s1r, ds, dr, fs, fr, us, ur, rs, rr, tss, trs, sas, credit):
    n, half, part, planes = p.n, p.half, p.part, p.planes
    send, back, gath = (s0, s1, s2), (r0, r1, r2), (g0, g1, g2)
    me, core = lax.axis_index("expert"), lax.axis_index("etp")
    at = (me // (n * n), lax.rem(me // n, n), lax.rem(me, n))
    stride = (n * n, n, 1)

    def device(d, sign=1):
        c = [lax.rem(v + (sign * o) % n, n) for v, o in zip(at, d)]
        return (c[0] * stride[0] + c[1] * stride[1] + c[2], core)

    partner = (me, 1 - core)

    def block_of(d):
        return device(d, -1)[0]

    own = pl.multiple_of(core * half, 128)
    other = pl.multiple_of((1 - core) * half, 128)
    loads = [
        pltpu.make_async_copy(dn_ref.at[:, :, pl.ds(own, half)], dno, wsem.at[0]),
        pltpu.make_async_copy(dn_ref.at[:, :, pl.ds(other, half)], dnp, wsem.at[1]),
        pltpu.make_async_copy(gw_ref.at[:, pl.ds(other, half), :], gwp, wsem.at[2]),
        pltpu.make_async_copy(uw_ref.at[:, pl.ds(other, half), :], uwp, wsem.at[3]),
        pltpu.make_async_copy(gw_ref.at[:, pl.ds(own, half), :], gwo, wsem.at[4]),
        pltpu.make_async_copy(uw_ref.at[:, pl.ds(own, half), :], uwo, wsem.at[5]),
    ]
    for load in loads:
        load.start()

    def saved_start(t):
        first, count = p.tiles[t]
        for j in range(count):
            b = block_of(p.order[first + j])
            pltpu.make_async_copy(sg_ref.at[b], sgt.at[j], sas.at[0]).start()
            pltpu.make_async_copy(su_ref.at[b], sut.at[j], sas.at[1]).start()

    def saved_wait(t):
        count = p.tiles[t][1]
        pltpu.make_async_copy(sg_ref.at[pl.ds(0, count)], sgt.at[pl.ds(0, count)], sas.at[0]).wait()
        pltpu.make_async_copy(su_ref.at[pl.ds(0, count)], sut.at[pl.ds(0, count)], sas.at[1]).wait()

    saved_start(0)

    barrier = pltpu.get_barrier_semaphore()
    for d in p.peers:
        pl.semaphore_signal(barrier, inc=1, device_id=device(d), device_id_type=MESH)
    pl.semaphore_signal(barrier, inc=1, device_id=partner, device_id_type=MESH)

    meta[...] = jnp.concatenate(
        [ids_ref[...].astype(F32), cw_ref[...].astype(F32)], axis=0
    ).astype(BF16)
    tokens = meta.shape[1]
    before = (
        lax.broadcasted_iota(I32, (tokens, tokens), 0)
        < lax.broadcasted_iota(I32, (tokens, tokens), 1)
    ).astype(F32).astype(BF16)
    rows = 2 * planes
    r_iota = lax.broadcasted_iota(I32, (rows, tokens), 0)

    def experts_of(f):
        a, b, c = AXES[f]
        place = r_iota // 2
        vb = lax.rem(at[b] + place // n, n)
        vc = lax.rem(at[c] + lax.rem(place, n), n)
        return 2 * (at[a] * stride[a] + vb * stride[b] + vc * stride[c]) + lax.rem(r_iota, 2)

    experts = [experts_of(f).astype(F32) for f in range(3)]
    c_iota = lax.broadcasted_iota(I32, (rows, CAP, tokens), 1).astype(F32)

    def select(f, a, info, token_cols):
        info = info.astype(F32)
        match = jnp.zeros((rows, tokens), F32)
        weight = jnp.zeros((rows, tokens), F32)
        for k in range(p.top):
            hit = experts[f] == info[k:k + 1, :]
            match = jnp.where(hit, 1.0, match)
            weight = jnp.where(hit, info[p.top + k:p.top + k + 1, :], weight)
        position = jnp.dot(match.astype(BF16), before, preferred_element_type=F32)
        code = jnp.where(match > 0, position, -1.0)
        codes[f, a] = code
        cws[f, a] = weight
        hot = jnp.where(code[:, None, :] == c_iota, 1.0, 0.0)
        hot = hot.reshape(rows * CAP, tokens).astype(BF16)
        width = p.widths[f]
        own_slot = p.slot[p.along(f, (a, 0, 0))]
        for lo in range(0, width, 256):
            hi = min(lo + 256, width)
            picked = jnp.dot(hot, token_cols(lo, hi), preferred_element_type=F32).astype(BF16)
            picked = picked.reshape(planes, 2, CAP, hi - lo)
            send[f][a, :, :, :, lo:hi] = picked
            xo[own_slot, :, :, f * part + lo:f * part + hi] = picked[0]

    def dispatch_copy(f, a, q):
        b, c = q // n, q % n
        width = p.widths[f]
        slot = p.slot[p.along(f, (a, b, c))]
        return pltpu.make_async_remote_copy(
            src_ref=send[f].at[a, q],
            dst_ref=xo.at[slot, :, :, pl.ds(f * part, width)],
            send_sem=ds.at[f, a],
            recv_sem=dr.at[f, slot],
            device_id=device(p.along(f, (0, b, c))),
            device_id_type=MESH,
        )

    def gather_copies(f, o):
        to = device(p.along(f, (o, 0, 0)))
        return (
            pltpu.make_async_remote_copy(
                src_ref=go_ref.at[:, pl.ds(f * part, p.widths[f])],
                dst_ref=gath[f].at[o - 1],
                send_sem=s1s.at[f, o - 1, 0], recv_sem=s1r.at[f, o - 1, 0],
                device_id=to, device_id_type=MESH),
            pltpu.make_async_remote_copy(
                src_ref=meta, dst_ref=gm.at[f, o - 1],
                send_sem=s1s.at[f, o - 1, 1], recv_sem=s1r.at[f, o - 1, 1],
                device_id=to, device_id_type=MESH),
        )

    pl.semaphore_wait(barrier, len(p.peers) + 1)
    for o in range(1, n):
        for f in range(3):
            for copy in gather_copies(f, o):
                copy.start()
    for f in range(3):
        select(f, 0, meta[...], lambda lo, hi: go_ref[:, f * part + lo:f * part + hi])
        for q in range(1, planes):
            dispatch_copy(f, 0, q).start()
    for a in range(1, n):
        for f in range(3):
            for copy in gather_copies(f, a):
                copy.wait_recv()
            select(f, a, gm[f, a - 1], lambda lo, hi: gath[f][a - 1, :, lo:hi])
            for q in range(1, planes):
                dispatch_copy(f, a, q).start()

    def forward_copy(t, lo, count):
        return pltpu.make_async_remote_copy(
            src_ref=xo.at[pl.ds(lo, count), :, :, pl.ds(0, half)],
            dst_ref=xp.at[pl.ds(lo, count), :, :, pl.ds(0, half)],
            send_sem=fs.at[t], recv_sem=fr.at[t],
            device_id=partner, device_id_type=MESH)

    def return_copy(f, t, slot):
        a, b, c = p.seen(f, p.order[slot])
        return pltpu.make_async_remote_copy(
            src_ref=xo.at[slot, :, :, pl.ds(f * part, part)],
            dst_ref=back[f].at[a, b * n + c],
            send_sem=rs.at[f, t], recv_sem=rr.at[f, a],
            device_id=device(p.along(f, (0, b, c)), -1), device_id_type=MESH)

    for t, (first, count) in enumerate(p.tiles):
        m = count * CAP
        for slot in range(first, first + count):
            for f in range(3):
                a, b, c = p.seen(f, p.order[slot])
                if (b, c) != (0, 0):
                    dispatch_copy(f, a, b * n + c).wait_recv()
            forward_copy(t, slot, 1).start()
        saved_wait(t)
        if t == 0:
            loads[0].wait()
            loads[1].wait()
        forward_copy(t, first, count).wait_recv()
        if t == 0:
            for load in loads[2:]:
                load.wait()

        def hidden(l, _):
            x_own = xo[pl.ds(first, count), l, :, 0:half].reshape(m, half)
            x_oth = xp[pl.ds(first, count), l, :, 0:half].reshape(m, half)
            g = lax.dot_general(x_own, dno[l], NT, preferred_element_type=F32)
            g = g + lax.dot_general(x_oth, dnp[l], NT, preferred_element_type=F32)
            gbuf[0:m, :] = g

            def pointwise(j, _):
                at_row = pl.ds(pl.multiple_of(j * CAP, CAP), CAP)
                grad = gbuf[at_row, :]
                gate = sgt[j, l].astype(F32)
                up = sut[j, l].astype(F32)
                sig = 0.5 * jnp.tanh(0.5 * gate) + 0.5
                act = gate * sig
                gup = grad * act
                total = jnp.sum(gup * up, axis=1, keepdims=True)
                xp[first + j, l, :, half:half + 128] = jnp.broadcast_to(total, (CAP, 128)).astype(BF16)
                ggb[l, at_row, :] = (grad * up * sig * (1.0 + gate * (1.0 - sig))).astype(BF16)
                gub[l, at_row, :] = gup.astype(BF16)
                return 0

            lax.fori_loop(0, count, pointwise, 0)
            project(l, gwp, uwp, xp)
            return 0

        def project(l, gate_w, up_w, into):
            gg, gu = ggb[l, 0:m, :], gub[l, 0:m, :]
            for lo in range(0, half, p.step):
                u = lax.dot_general(gg, gate_w[l, lo:lo + p.step, :], NT, preferred_element_type=F32)
                u = u + lax.dot_general(gu, up_w[l, lo:lo + p.step, :], NT, preferred_element_type=F32)
                into[pl.ds(first, count), l, :, lo:lo + p.step] = u.astype(BF16).reshape(count, CAP, p.step)

        lax.fori_loop(0, 2, hidden, 0)
        if t + 1 < len(p.tiles):
            saved_start(t + 1)
        if t > 0:
            pl.semaphore_wait(credit, 1)
        swap = pltpu.make_async_remote_copy(
            src_ref=xp.at[pl.ds(first, count)], dst_ref=uin.at[pl.ds(0, count)],
            send_sem=us.at[t], recv_sem=ur.at[t], device_id=partner, device_id_type=MESH)
        swap.start()
        forward_copy(t, first, count).wait_send()

        def keep(l, _):
            project(l, gwo, uwo, xo)
            xo[pl.ds(first, count), l, :, half:half + 128] = xp[pl.ds(first, count), l, :, half:half + 128]
            return 0

        lax.fori_loop(0, 2, keep, 0)
        swap.wait_recv()

        def add(j, _):
            xo[first + j] = (xo[first + j].astype(F32) + uin[j].astype(F32)).astype(BF16)
            return 0

        lax.fori_loop(0, count, add, 0)
        if t + 1 < len(p.tiles):
            pl.semaphore_signal(credit, inc=1, device_id=partner, device_id_type=MESH)
        for slot in range(first, first + count):
            for f in range(3):
                a, b, c = p.seen(f, p.order[slot])
                if (b, c) == (0, 0):
                    back[f][a, 0] = xo[slot, :, :, f * part:(f + 1) * part]
                else:
                    return_copy(f, t, slot).start()

    def total_copy(f, o):
        to = device(p.along(f, (o, 0, 0)), -1)
        width = p.widths[f]
        copies = [pltpu.make_async_remote_copy(
            src_ref=ts.at[f, o - 1, :, pl.ds(0, width)], dst_ref=tr.at[f, o - 1, :, pl.ds(0, width)],
            send_sem=tss.at[f, o - 1, 0], recv_sem=trs.at[f, o - 1, 0],
            device_id=to, device_id_type=MESH)]
        if f == 2:
            copies.append(pltpu.make_async_remote_copy(
                src_ref=gcs.at[o - 1], dst_ref=gcr.at[o - 1],
                send_sem=tss.at[f, o - 1, 1], recv_sem=trs.at[f, o - 1, 1],
                device_id=to, device_id_type=MESH))
        return copies

    def back_wait(f, a):
        pltpu.make_async_remote_copy(
            src_ref=xo.at[pl.ds(0, planes - 1), :, :, pl.ds(0, part)],
            dst_ref=back[f].at[a, pl.ds(1, planes - 1)],
            send_sem=rs.at[f, 0], recv_sem=rr.at[f, a],
            device_id=partner, device_id_type=MESH).wait_recv()

    def combined(f, a, info):
        back_wait(f, a)
        hit = codes[f, a][:, None, :] == c_iota
        weight = jnp.where(hit, cws[f, a][:, None, :], 0.0)
        weight = weight.reshape(rows * CAP, tokens).astype(BF16)
        width = p.widths[f]
        values = back[f][a, :, :, :, 0:width].reshape(rows * CAP, width)
        total = lax.dot_general(weight, values, TN, preferred_element_type=F32)
        if f < 2:
            return total, None
        hot = jnp.where(hit, 1.0, 0.0).reshape(rows * CAP, tokens).astype(BF16)
        sums = back[f][a, :, :, :, width:part].reshape(rows * CAP, 128)
        lane = lax.broadcasted_iota(I32, (rows * CAP, 128), 1)
        row = lax.broadcasted_iota(I32, (rows * CAP, 128), 0) // CAP
        sums = jnp.where(lane == row, sums.astype(F32), 0.0).astype(BF16)
        spread = lax.dot_general(sums, hot, TN, preferred_element_type=F32)[0:rows]
        info = info.astype(F32)
        picked = [
            jnp.sum(jnp.where(experts[f] == info[k:k + 1, :], spread, 0.0), axis=0, keepdims=True)
            for k in range(p.top)
        ]
        return total, jnp.concatenate(picked, axis=0)

    for a in range(1, n):
        for f in range(3):
            total, sums = combined(f, a, gm[f, a - 1])
            ts[f, a - 1, :, 0:p.widths[f]] = total.astype(BF16)
            if f == 2:
                gcs[a - 1] = sums
            for copy in total_copy(f, a):
                copy.start()
    for f in range(3):
        total, sums = combined(f, 0, meta[...])
        width = p.widths[f]
        for a in range(1, n):
            for copy in total_copy(f, a):
                copy.wait_recv()
            total = total + tr[f, a - 1, :, 0:width].astype(F32)
            if f == 2:
                sums = sums + gcr[a - 1]
        gt_ref[:, f * part:f * part + width] = total.astype(BF16)
        if f == 2:
            gc_ref[...] = sums.astype(BF16)

    for f in range(3):
        width = p.widths[f]
        for o in range(1, n):
            for copy in gather_copies(f, o) + tuple(total_copy(f, o)):
                copy.wait_send()
        for a in range(n):
            pltpu.make_async_remote_copy(
                src_ref=send[f].at[a, pl.ds(1, planes - 1)],
                dst_ref=send[f].at[a, pl.ds(1, planes - 1)],
                send_sem=ds.at[f, a], recv_sem=dr.at[f, 0],
                device_id=partner, device_id_type=MESH).wait_send()
        for t, (first, count) in enumerate(p.tiles):
            sent = sum(p.seen(f, p.order[s])[1:] != (0, 0) for s in range(first, first + count))
            if sent:
                pltpu.make_async_remote_copy(
                    src_ref=xo.at[pl.ds(0, sent), :, :, pl.ds(0, part)],
                    dst_ref=xp.at[pl.ds(0, sent), :, :, pl.ds(0, part)],
                    send_sem=rs.at[f, t], recv_sem=rr.at[f, 0],
                    device_id=partner, device_id_type=MESH).wait_send()
    for t, (first, count) in enumerate(p.tiles):
        pltpu.make_async_remote_copy(
            src_ref=xp.at[pl.ds(first, count)], dst_ref=uin.at[pl.ds(0, count)],
            send_sem=us.at[t], recv_sem=ur.at[t], device_id=partner, device_id_type=MESH).wait_send()


def on_device(plan, grad_out, combine, expert_ids, saved_gate, saved_up, gate_weight, up_weight, down_weight):
    p = plan
    n, half, ff, part, planes = p.n, p.half, p.ff, p.part, p.planes
    tokens, top = expert_ids.shape
    blocks, nt = n * n * n, len(p.tiles)
    saved = [
        jnp.transpose(v.reshape(blocks, CAP, 2, ff), (0, 2, 1, 3)) for v in (saved_gate, saved_up)
    ]
    vmem = pl.BlockSpec(memory_space=pltpu.VMEM)
    hbm = pl.BlockSpec(memory_space=pl.ANY)
    dma, regular = pltpu.SemaphoreType.DMA, pltpu.SemaphoreType.REGULAR
    rows = 2 * planes
    scratch = [
        pltpu.VMEM((blocks, 2, CAP, p.wide), BF16),
        pltpu.VMEM((blocks, 2, CAP, p.wide), BF16),
        pltpu.VMEM((p.most, 2, CAP, p.wide), BF16),
        *[pltpu.VMEM((n, planes, 2, CAP, w), BF16) for w in p.widths],
        *[pltpu.VMEM((n, planes, 2, CAP, part), BF16) for _ in range(3)],
        *[pltpu.VMEM((n - 1, tokens, w), BF16) for w in p.widths],
        pltpu.VMEM((3, n - 1, 2 * top, tokens), BF16),
        pltpu.VMEM((3, n - 1, tokens, part), BF16),
        pltpu.VMEM((3, n - 1, tokens, part), BF16),
        pltpu.VMEM((n - 1, top, tokens), F32),
        pltpu.VMEM((n - 1, top, tokens), F32),
        pltpu.VMEM((3, n, rows, tokens), F32),
        pltpu.VMEM((3, n, rows, tokens), F32),
        pltpu.VMEM((2 * top, tokens), BF16),
        pltpu.VMEM((2, ff, half), BF16),
        pltpu.VMEM((2, ff, half), BF16),
        *[pltpu.VMEM((2, half, ff), BF16) for _ in range(4)],
        pltpu.VMEM((p.most, 2, CAP, ff), BF16),
        pltpu.VMEM((p.most, 2, CAP, ff), BF16),
        pltpu.VMEM((p.most * CAP, ff), F32),
        pltpu.VMEM((2, p.most * CAP, ff), BF16),
        pltpu.VMEM((2, p.most * CAP, ff), BF16),
        dma((6,)), dma((3, n - 1, 2)), dma((3, n - 1, 2)), dma((3, n)), dma((3, blocks)),
        dma((nt,)), dma((nt,)), dma((nt,)), dma((nt,)), dma((3, nt)), dma((3, n)),
        dma((3, n - 1, 2)), dma((3, n - 1, 2)), dma((2,)), regular,
    ]
    grad_tokens, grad_combine = pl.pallas_call(
        functools.partial(kernel, p),
        out_shape=(
            jax.ShapeDtypeStruct((tokens, half), BF16),
            jax.ShapeDtypeStruct((top, tokens), BF16),
        ),
        in_specs=[vmem, vmem, vmem, hbm, hbm, hbm, hbm, hbm],
        out_specs=(vmem, vmem),
        scratch_shapes=scratch,
        compiler_params=pltpu.CompilerParams(
            collective_id=0, has_side_effects=True, vmem_limit_bytes=67043328
        ),
    )(expert_ids.T, combine.T, grad_out, *saved, gate_weight, up_weight, down_weight)
    return grad_tokens, grad_combine.T


def solution(mesh, tiles=(8, 19, 19, 18), step=256):
    n = round(mesh.shape["expert"] ** (1 / 3))

    def run(grad_out, combine, expert_ids, saved_gate, saved_up, gate_weight, up_weight, down_weight):
        plan = Plan(n, grad_out.shape[1], gate_weight.shape[2], expert_ids.shape[1], tiles, step)
        return on_device(
            plan, grad_out, combine, expert_ids, saved_gate, saved_up, gate_weight, up_weight, down_weight
        )

    in_specs = (
        P("expert", "etp"),
        P("expert", None),
        P("expert", None),
        P(None, "expert", "etp"),
        P(None, "expert", "etp"),
        P("expert", None, "etp"),
        P("expert", None, "etp"),
        P("expert", "etp", None),
    )
    out_specs = (P("expert", "etp"), P("expert", None))
    return jax.shard_map(run, mesh=mesh, in_specs=in_specs, out_specs=out_specs, check_vma=False)
```

time: 434 us -> 193 us (0.44)
  the two profiles are of different devices: /device:TPU:34 before, /device:TPU:1 now
where the time goes in v1:
time: 193 us
  Pallas kernels  184 us (95%)
  local copies, waits for them, and re-layouts  8.38 us (4%)
    pallas_call x1, Pallas kernels, on_device(): pl.pallas_call(functools.partial(kernel, p), out_shape=(jax.ShapeDtypeStr...  184 us
    transpose x1, local copies, waits for them, and re-layouts, on_device(): jnp.transpose(v.reshape(blocks, CAP, 2, ff), (0, 2, 1, 3))  5.31 us

profile of v1, /device:TPU:1, one launch (start us, length us, event | category | flops | bytes accessed | tf_op | source)
XLA Modules:
  0.0 192.7 jit_solution(12005147985084518874)
XLA Ops:
  0.6 5.3 %copy_bitcast_fusion = (bf16[64,2,16,512]{3,2,1,0:T(8,128)(2,1)}, bf16[64,2,16,512]{3,2,1,0:T(8,128)(2,1)}) fusion(bf16[64,16,2,512]{3,2,1,0:T(2,128)(2,1)} %bitcast.9, bf16[64,16,2,512]{3,2,1,0:T(2,128)(2,1)} %bitcast.10), kind=kLoop, calls=%fused_computation | loop fusion | bytes 8388608 | tf_op jit(solution)/shard_map/transpose | solution.py:378
  5.9 183.7 %shard_map.95 = (bf16[128,1792]{1,0:T(8,128)(2,1)}, bf16[8,128]{1,0:T(8,128)(2,1)}) custom-call(s32[8,128]{1,0:T(8,128)} %bitcast.11, bf16[8,128]{1,0:T(8,128)(2,1)} %bitcast.12, bf16[128,1792]{1,0:T(8,128)(2,1)} %go_ref.1, bf16[64,2,16,512]{3,2,1,0:T(8,128)(2,1)} %get-tuple-element.7.sg_ref, bf16[64,2,16,512]{3,2,1,0:T(8,128)(2,1)} %get-tuple-element.6.su_ref, ...), custom_call_target="tpu_custom_call" | custom-call | tf_op jit(solution)/shard_map/pallas_call | solution.py:411
  189.6 1.8 copy.22
  191.4 1.3 copy.23

commit v2 on v1

--- a/solution.py
+++ b/solution.py
@@ -22,13 +22,16 @@
         self.part = (half + 128) // 3
         self.wide = 3 * self.part
         self.widths = (self.part, self.part, self.part - 128)
-        self.order = sorted(itertools.product(range(n), repeat=3), key=lambda d: (max(d), d))
+        far = lambda d: tuple(min(v, n - v) for v in d)
+        self.order = sorted(itertools.product(range(n), repeat=3), key=lambda d: (max(far(d)), sum(d) % 2, d))
         self.slot = {d: i for i, d in enumerate(self.order)}
         self.tiles, start = [], 0
         for count in tiles:
             self.tiles.append((start, count))
             start += count
         self.most = max(tiles)
+        self.tile = [t for t, count in enumerate(tiles) for _ in range(count)]
+        self.offsets = sorted(range(1, n), key=lambda o: min(o, n - o))
         self.planes = n * n
         self.peers = [d for d in self.order if 0 < sum(v > 0 for v in d) < 3]
 
@@ -43,9 +46,9 @@
 
 
 def kernel(p, ids_ref, cw_ref, go_ref, sg_ref, su_ref, gw_ref, uw_ref, dn_ref, gt_ref, gc_ref,
-           xo, xp, uin, s0, s1, s2, r0, r1, r2, g0, g1, g2, gm, ts, tr, gcs, gcr, codes, cws, meta,
-           dno, dnp, gwo, gwp, uwo, uwp, sgt, sut, gbuf, ggb, gub,
-           wsem, s1s, s1r, ds, dr, fs, fr, us, ur, rs, rr, tss, trs, sas, credit):
+           xo, s0, s1, s2, r0, r1, r2, g0, g1, g2, gm, ts, tr, gcs, gcr, codes, cws, meta,
+           dna, dnb, gwa, gwb, uwa, uwb, sgt, sut, gbuf, pout, pin, hout, hin,
+           wsem, wss, wsr, s1s, s1r, ds, dr, ps, pr, hs, hr, rs, rr, tss, trs, sas):
     n, half, part, planes = p.n, p.half, p.part, p.planes
     send, back, gath = (s0, s1, s2), (r0, r1, r2), (g0, g1, g2)
     me, core = lax.axis_index("expert"), lax.axis_index("etp")
@@ -64,15 +67,22 @@
     own = pl.multiple_of(core * half, 128)
     other = pl.multiple_of((1 - core) * half, 128)
     loads = [
-        pltpu.make_async_copy(dn_ref.at[:, :, pl.ds(own, half)], dno, wsem.at[0]),
-        pltpu.make_async_copy(dn_ref.at[:, :, pl.ds(other, half)], dnp, wsem.at[1]),
-        pltpu.make_async_copy(gw_ref.at[:, pl.ds(other, half), :], gwp, wsem.at[2]),
-        pltpu.make_async_copy(uw_ref.at[:, pl.ds(other, half), :], uwp, wsem.at[3]),
-        pltpu.make_async_copy(gw_ref.at[:, pl.ds(own, half), :], gwo, wsem.at[4]),
-        pltpu.make_async_copy(uw_ref.at[:, pl.ds(own, half), :], uwo, wsem.at[5]),
+        pltpu.make_async_copy(dn_ref.at[:, :, pl.ds(own, half)], dna, wsem.at[0]),
+        pltpu.make_async_copy(gw_ref.at[:, pl.ds(own, half), :], gwa, wsem.at[1]),
+        pltpu.make_async_copy(uw_ref.at[:, pl.ds(own, half), :], uwa, wsem.at[2]),
     ]
     for load in loads:
         load.start()
+    trades = [
+        pltpu.make_async_remote_copy(
+            src_ref=src, dst_ref=dst, send_sem=wss.at[i], recv_sem=wsr.at[i],
+            device_id=partner, device_id_type=MESH)
+        for i, (src, dst) in enumerate((
+            (dn_ref.at[:, :, pl.ds(other, half)], dnb),
+            (gw_ref.at[:, pl.ds(other, half), :], gwb),
+            (uw_ref.at[:, pl.ds(other, half), :], uwb),
+        ))
+    ]
 
     def saved_start(t):
         first, count = p.tiles[t]
@@ -144,7 +154,7 @@
         return pltpu.make_async_remote_copy(
             src_ref=send[f].at[a, q],
             dst_ref=xo.at[slot, :, :, pl.ds(f * part, width)],
-            send_sem=ds.at[f, a],
+            send_sem=ds.at[f, p.tile[slot], a],
             recv_sem=dr.at[f, slot],
             device_id=device(p.along(f, (0, b, c))),
             device_id_type=MESH,
@@ -164,29 +174,21 @@
                 device_id=to, device_id_type=MESH),
         )
 
-    pl.semaphore_wait(barrier, len(p.peers) + 1)
-    for o in range(1, n):
-        for f in range(3):
-            for copy in gather_copies(f, o):
-                copy.start()
-    for f in range(3):
-        select(f, 0, meta[...], lambda lo, hi: go_ref[:, f * part + lo:f * part + hi])
-        for q in range(1, planes):
-            dispatch_copy(f, 0, q).start()
-    for a in range(1, n):
-        for f in range(3):
-            for copy in gather_copies(f, a):
-                copy.wait_recv()
-            select(f, a, gm[f, a - 1], lambda lo, hi: gath[f][a - 1, :, lo:hi])
-            for q in range(1, planes):
-                dispatch_copy(f, a, q).start()
-
-    def forward_copy(t, lo, count):
-        return pltpu.make_async_remote_copy(
-            src_ref=xo.at[pl.ds(lo, count), :, :, pl.ds(0, half)],
-            dst_ref=xp.at[pl.ds(lo, count), :, :, pl.ds(0, half)],
-            send_sem=fs.at[t], recv_sem=fr.at[t],
-            device_id=partner, device_id_type=MESH)
+    def dispatch(f, a, t):
+        return [q for q in range(1, planes)
+                if p.tile[p.slot[p.along(f, (a, q // n, q % n))]] == t]
+
+    def dispatch_start(f, a, t):
+        for q in dispatch(f, a, t):
+            dispatch_copy(f, a, q).start()
+
+    def dispatch_sent(f, a, t):
+        k = len(dispatch(f, a, t))
+        if k:
+            pltpu.make_async_remote_copy(
+                src_ref=send[f].at[a, pl.ds(0, k)], dst_ref=send[f].at[a, pl.ds(0, k)],
+                send_sem=ds.at[f, t, a], recv_sem=dr.at[f, 0],
+                device_id=partner, device_id_type=MESH).wait_send()
 
     def return_copy(f, t, slot):
         a, b, c = p.seen(f, p.order[slot])
@@ -196,6 +198,29 @@
             send_sem=rs.at[f, t], recv_sem=rr.at[f, a],
             device_id=device(p.along(f, (0, b, c)), -1), device_id_type=MESH)
 
+    last = len(p.tiles) - 1
+    pl.semaphore_wait(barrier, len(p.peers) + 1)
+    for o in p.offsets:
+        for f in range(3):
+            for copy in gather_copies(f, o):
+                copy.start()
+    for trade in trades:
+        trade.start()
+    for f in range(3):
+        select(f, 0, meta[...], lambda lo, hi: go_ref[:, f * part + lo:f * part + hi])
+        dispatch_start(f, 0, 0)
+    for a in p.offsets:
+        for f in range(3):
+            for copy in gather_copies(f, a):
+                copy.wait_recv()
+            select(f, a, gm[f, a - 1], lambda lo, hi: gath[f][a - 1, :, lo:hi])
+            dispatch_start(f, a, 0)
+    for a in [0] + p.offsets:
+        for f in range(3):
+            dispatch_sent(f, a, 0)
+            if last >= 1:
+                dispatch_start(f, a, 1)
+
     for t, (first, count) in enumerate(p.tiles):
         m = count * CAP
         for slot in range(first, first + count):
@@ -203,74 +228,98 @@
                 a, b, c = p.seen(f, p.order[slot])
                 if (b, c) != (0, 0):
                     dispatch_copy(f, a, b * n + c).wait_recv()
-            forward_copy(t, slot, 1).start()
-        saved_wait(t)
         if t == 0:
             loads[0].wait()
-            loads[1].wait()
-        forward_copy(t, first, count).wait_recv()
+            trades[0].wait_recv()
+
+        def part_copy(l):
+            return pltpu.make_async_remote_copy(
+                src_ref=pout.at[l, pl.ds(0, m)], dst_ref=pin.at[l, pl.ds(0, m)],
+                send_sem=ps.at[l], recv_sem=pr.at[l], device_id=partner, device_id_type=MESH)
+
+        def hidden_copy(l):
+            return pltpu.make_async_remote_copy(
+                src_ref=hout.at[l, pl.ds(0, m)], dst_ref=hin.at[l, pl.ds(0, m)],
+                send_sem=hs.at[l], recv_sem=hr.at[l], device_id=partner, device_id_type=MESH)
+
+        def features(l):
+            return xo[pl.ds(first, count), l, :, 0:half].reshape(m, half)
+
+        def part_of_other(l, _):
+            pout[l, 0:m, :] = lax.dot_general(features(l), dnb[l], NT, preferred_element_type=F32)
+            part_copy(l).start()
+            return 0
+
+        def part_of_own(l, _):
+            gbuf[l, 0:m, :] = lax.dot_general(features(l), dna[l], NT, preferred_element_type=F32)
+            return 0
+
+        def pointwise(l, at_row, j):
+            grad = gbuf[l, at_row, :] + pin[l, at_row, :]
+            gate = sgt[j, l].astype(F32)
+            up = sut[j, l].astype(F32)
+            sig = 0.5 * jnp.tanh(0.5 * gate) + 0.5
+            act = gate * sig
+            gup = grad * act
+            total = jnp.sum(gup * up, axis=1, keepdims=True)
+            hout[l, at_row, 0:p.ff] = (grad * up * sig * (1.0 + gate * (1.0 - sig))).astype(BF16)
+            hout[l, at_row, p.ff:2 * p.ff] = gup.astype(BF16)
+            hout[l, at_row, 2 * p.ff:] = jnp.broadcast_to(total, (CAP, 128)).astype(BF16)
+
+        def hidden(l, _):
+            part_copy(l).wait_recv()
+
+            def two(i, _):
+                for k in range(2):
+                    j = 2 * i + k
+                    pointwise(l, pl.ds(pl.multiple_of(j * CAP, CAP), CAP), j)
+                return 0
+
+            lax.fori_loop(0, count // 2, two, 0)
+            if count % 2:
+                pointwise(l, pl.ds((count - 1) * CAP, CAP), count - 1)
+            hidden_copy(l).start()
+            return 0
+
+        def project(l, _):
+            hidden_copy(l).wait_recv()
+            sums = hout[l, 0:m, 2 * p.ff:].astype(F32) + hin[l, 0:m, 2 * p.ff:].astype(F32)
+            xo[pl.ds(first, count), l, :, half:half + 128] = sums.astype(BF16).reshape(count, CAP, 128)
+            for lo in range(0, half, p.step):
+                u = None
+                for h, gate_w, up_w in ((hout, gwa, uwa), (hin, gwb, uwb)):
+                    for at_col, w in ((0, gate_w), (p.ff, up_w)):
+                        term = lax.dot_general(
+                            h[l, 0:m, at_col:at_col + p.ff], w[l, lo:lo + p.step, :], NT,
+                            preferred_element_type=F32)
+                        u = term if u is None else u + term
+                xo[pl.ds(first, count), l, :, lo:lo + p.step] = u.astype(BF16).reshape(count, CAP, p.step)
+            return 0
+
+        def sent(copy):
+            def wait(l, _):
+                copy(l).wait_send()
+                return 0
+            lax.fori_loop(0, 2, wait, 0)
+
+        lax.fori_loop(0, 2, part_of_other, 0)
+        lax.fori_loop(0, 2, part_of_own, 0)
+        saved_wait(t)
+        lax.fori_loop(0, 2, hidden, 0)
+        if t < last:
+            saved_start(t + 1)
         if t == 0:
-            for load in loads[2:]:
+            for load in loads[1:]:
                 load.wait()
-
-        def hidden(l, _):
-            x_own = xo[pl.ds(first, count), l, :, 0:half].reshape(m, half)
-            x_oth = xp[pl.ds(first, count), l, :, 0:half].reshape(m, half)
-            g = lax.dot_general(x_own, dno[l], NT, preferred_element_type=F32)
-            g = g + lax.dot_general(x_oth, dnp[l], NT, preferred_element_type=F32)
-            gbuf[0:m, :] = g
-
-            def pointwise(j, _):
-                at_row = pl.ds(pl.multiple_of(j * CAP, CAP), CAP)
-                grad = gbuf[at_row, :]
-                gate = sgt[j, l].astype(F32)
-                up = sut[j, l].astype(F32)
-                sig = 0.5 * jnp.tanh(0.5 * gate) + 0.5
-                act = gate * sig
-                gup = grad * act
-                total = jnp.sum(gup * up, axis=1, keepdims=True)
-                xp[first + j, l, :, half:half + 128] = jnp.broadcast_to(total, (CAP, 128)).astype(BF16)
-                ggb[l, at_row, :] = (grad * up * sig * (1.0 + gate * (1.0 - sig))).astype(BF16)
-                gub[l, at_row, :] = gup.astype(BF16)
-                return 0
-
-            lax.fori_loop(0, count, pointwise, 0)
-            project(l, gwp, uwp, xp)
-            return 0
-
-        def project(l, gate_w, up_w, into):
-            gg, gu = ggb[l, 0:m, :], gub[l, 0:m, :]
-            for lo in range(0, half, p.step):
-                u = lax.dot_general(gg, gate_w[l, lo:lo + p.step, :], NT, preferred_element_type=F32)
-                u = u + lax.dot_general(gu, up_w[l, lo:lo + p.step, :], NT, preferred_element_type=F32)
-                into[pl.ds(first, count), l, :, lo:lo + p.step] = u.astype(BF16).reshape(count, CAP, p.step)
-
-        lax.fori_loop(0, 2, hidden, 0)
-        if t + 1 < len(p.tiles):
-            saved_start(t + 1)
-        if t > 0:
-            pl.semaphore_wait(credit, 1)
-        swap = pltpu.make_async_remote_copy(
-            src_ref=xp.at[pl.ds(first, count)], dst_ref=uin.at[pl.ds(0, count)],
-            send_sem=us.at[t], recv_sem=ur.at[t], device_id=partner, device_id_type=MESH)
-        swap.start()
-        forward_copy(t, first, count).wait_send()
-
-        def keep(l, _):
-            project(l, gwo, uwo, xo)
-            xo[pl.ds(first, count), l, :, half:half + 128] = xp[pl.ds(first, count), l, :, half:half + 128]
-            return 0
-
-        lax.fori_loop(0, 2, keep, 0)
-        swap.wait_recv()
-
-        def add(j, _):
-            xo[first + j] = (xo[first + j].astype(F32) + uin[j].astype(F32)).astype(BF16)
-            return 0
-
-        lax.fori_loop(0, count, add, 0)
-        if t + 1 < len(p.tiles):
-            pl.semaphore_signal(credit, inc=1, device_id=partner, device_id_type=MESH)
+            for trade in trades[1:]:
+                trade.wait_recv()
+        if 0 < t + 2 <= last:
+            for a in [0] + p.offsets:
+                for f in range(3):
+                    dispatch_start(f, a, t + 2)
+        lax.fori_loop(0, 2, project, 0)
+        sent(part_copy)
+        sent(hidden_copy)
         for slot in range(first, first + count):
             for f in range(3):
                 a, b, c = p.seen(f, p.order[slot])
@@ -323,7 +372,7 @@
         ]
         return total, jnp.concatenate(picked, axis=0)
 
-    for a in range(1, n):
+    for a in p.offsets:
         for f in range(3):
             total, sums = combined(f, a, gm[f, a - 1])
             ts[f, a - 1, :, 0:p.widths[f]] = total.astype(BF16)
@@ -349,24 +398,19 @@
         for o in range(1, n):
             for copy in gather_copies(f, o) + tuple(total_copy(f, o)):
                 copy.wait_send()
-        for a in range(n):
-            pltpu.make_async_remote_copy(
-                src_ref=send[f].at[a, pl.ds(1, planes - 1)],
-                dst_ref=send[f].at[a, pl.ds(1, planes - 1)],
-                send_sem=ds.at[f, a], recv_sem=dr.at[f, 0],
-                device_id=partner, device_id_type=MESH).wait_send()
         for t, (first, count) in enumerate(p.tiles):
+            if t > 0:
+                for a in range(n):
+                    dispatch_sent(f, a, t)
             sent = sum(p.seen(f, p.order[s])[1:] != (0, 0) for s in range(first, first + count))
             if sent:
                 pltpu.make_async_remote_copy(
                     src_ref=xo.at[pl.ds(0, sent), :, :, pl.ds(0, part)],
-                    dst_ref=xp.at[pl.ds(0, sent), :, :, pl.ds(0, part)],
+                    dst_ref=xo.at[pl.ds(0, sent), :, :, pl.ds(0, part)],
                     send_sem=rs.at[f, t], recv_sem=rr.at[f, 0],
                     device_id=partner, device_id_type=MESH).wait_send()
-    for t, (first, count) in enumerate(p.tiles):
-        pltpu.make_async_remote_copy(
-            src_ref=xp.at[pl.ds(first, count)], dst_ref=uin.at[pl.ds(0, count)],
-            send_sem=us.at[t], recv_sem=ur.at[t], device_id=partner, device_id_type=MESH).wait_send()
+    for trade in trades:
+        trade.wait_send()
 
 
 def on_device(plan, grad_out, combine, expert_ids, saved_gate, saved_up, gate_weight, up_weight, down_weight):
@@ -379,12 +423,10 @@
     ]
     vmem = pl.BlockSpec(memory_space=pltpu.VMEM)
     hbm = pl.BlockSpec(memory_space=pl.ANY)
-    dma, regular = pltpu.SemaphoreType.DMA, pltpu.SemaphoreType.REGULAR
+    dma = pltpu.SemaphoreType.DMA
     rows = 2 * planes
     scratch = [
         pltpu.VMEM((blocks, 2, CAP, p.wide), BF16),
-        pltpu.VMEM((blocks, 2, CAP, p.wide), BF16),
-        pltpu.VMEM((p.most, 2, CAP, p.wide), BF16),
         *[pltpu.VMEM((n, planes, 2, CAP, w), BF16) for w in p.widths],
         *[pltpu.VMEM((n, planes, 2, CAP, part), BF16) for _ in range(3)],
         *[pltpu.VMEM((n - 1, tokens, w), BF16) for w in p.widths],
@@ -401,12 +443,11 @@
         *[pltpu.VMEM((2, half, ff), BF16) for _ in range(4)],
         pltpu.VMEM((p.most, 2, CAP, ff), BF16),
         pltpu.VMEM((p.most, 2, CAP, ff), BF16),
-        pltpu.VMEM((p.most * CAP, ff), F32),
-        pltpu.VMEM((2, p.most * CAP, ff), BF16),
-        pltpu.VMEM((2, p.most * CAP, ff), BF16),
-        dma((6,)), dma((3, n - 1, 2)), dma((3, n - 1, 2)), dma((3, n)), dma((3, blocks)),
-        dma((nt,)), dma((nt,)), dma((nt,)), dma((nt,)), dma((3, nt)), dma((3, n)),
-        dma((3, n - 1, 2)), dma((3, n - 1, 2)), dma((2,)), regular,
+        *[pltpu.VMEM((2, p.most * CAP, ff), F32) for _ in range(3)],
+        *[pltpu.VMEM((2, p.most * CAP, 2 * ff + 128), BF16) for _ in range(2)],
+        dma((3,)), dma((3,)), dma((3,)), dma((3, n - 1, 2)), dma((3, n - 1, 2)),
+        dma((3, nt, n)), dma((3, blocks)), dma((2,)), dma((2,)), dma((2,)), dma((2,)),
+        dma((3, nt)), dma((3, n)), dma((3, n - 1, 2)), dma((3, n - 1, 2)), dma((2,)),
     ]
     grad_tokens, grad_combine = pl.pallas_call(
         functools.partial(kernel, p),
@@ -424,7 +465,7 @@
     return grad_tokens, grad_combine.T
 
 
-def solution(mesh, tiles=(8, 19, 19, 18), step=256):
+def solution(mesh, tiles=(27, 19, 18), step=256):
     n = round(mesh.shape["expert"] ** (1 / 3))
 
     def run(grad_out, combine, expert_ids, saved_gate, saved_up, gate_weight, up_weight, down_weight):

time: 193 us -> 159 us (0.82)
  Pallas kernels: 184 us -> 150 us
    pallas_call x1, Pallas kernels: 184 us -> 150 us  [on_device(): pl.pallas_call(functools.partial(kernel, p), out_shape=(jax.ShapeDtypeStr...]
where the time goes in v2:
time: 159 us
  Pallas kernels  150 us (94%)
  local copies, waits for them, and re-layouts  8.38 us (5%)
    pallas_call x1, Pallas kernels, on_device(): pl.pallas_call(functools.partial(kernel, p), out_shape=(jax.ShapeDtypeStr...  150 us
    transpose x1, local copies, waits for them, and re-layouts, on_device(): jnp.transpose(v.reshape(blocks, CAP, 2, ff), (0, 2, 1, 3))  5.31 us

profile of v2, /device:TPU:1, one launch (start us, length us, event | category | flops | bytes accessed | tf_op | source)
XLA Modules:
  0.0 159.3 jit_solution(18295424253913055817)
XLA Ops:
  0.6 5.3 %copy_bitcast_fusion = (bf16[64,2,16,512]{3,2,1,0:T(8,128)(2,1)}, bf16[64,2,16,512]{3,2,1,0:T(8,128)(2,1)}) fusion(bf16[64,16,2,512]{3,2,1,0:T(2,128)(2,1)} %bitcast.9, bf16[64,16,2,512]{3,2,1,0:T(2,128)(2,1)} %bitcast.10), kind=kLoop, calls=%fused_computation | loop fusion | bytes 8388608 | tf_op jit(solution)/shard_map/transpose | solution.py:422
  5.9 150.2 %shard_map.95 = (bf16[128,1792]{1,0:T(8,128)(2,1)}, bf16[8,128]{1,0:T(8,128)(2,1)}) custom-call(s32[8,128]{1,0:T(8,128)} %bitcast.11, bf16[8,128]{1,0:T(8,128)(2,1)} %bitcast.12, bf16[128,1792]{1,0:T(8,128)(2,1)} %go_ref.1, bf16[64,2,16,512]{3,2,1,0:T(8,128)(2,1)} %get-tuple-element.7.sg_ref, bf16[64,2,16,512]{3,2,1,0:T(8,128)(2,1)} %get-tuple-element.6.su_ref, ...), custom_call_target="tpu_custom_call" | custom-call | tf_op jit(solution)/shard_map/pallas_call | solution.py:452
  156.2 1.8 %copy.22 = bf16[128,1792]{1,0:T(8,128)(2,1)} copy(bf16[128,1792]{1,0:T(8,128)(2,1)} %get-tuple-element.10) | data formatting | bytes 917504
  158.0 1.3 copy.23

commit v3 on v2

--- a/solution.py
+++ b/solution.py
@@ -20,8 +20,7 @@
     def __init__(self, n, half, ff, top, tiles, step):
         self.n, self.half, self.ff, self.top, self.step = n, half, ff, top, step
         self.part = (half + 128) // 3
-        self.wide = 3 * self.part
-        self.widths = (self.part, self.part, self.part - 128)
+        self.base = (0, self.part, 2 * self.part - 128)
         far = lambda d: tuple(min(v, n - v) for v in d)
         self.order = sorted(itertools.product(range(n), repeat=3), key=lambda d: (max(far(d)), sum(d) % 2, d))
         self.slot = {d: i for i, d in enumerate(self.order)}
@@ -33,7 +32,25 @@
         self.tile = [t for t, count in enumerate(tiles) for _ in range(count)]
         self.offsets = sorted(range(1, n), key=lambda o: min(o, n - o))
         self.planes = n * n
+        self.kind, load = {}, [0, 0, 0]
+        for d in sorted(self.order, key=lambda d: -sum(far(d))):
+            choices = []
+            for kind in range(2):
+                new = list(load)
+                for f in range(3):
+                    lo, hi = self.span_of(f, kind)
+                    for axis in AXES[f][1:]:
+                        new[axis] += (hi - lo) * far(d)[axis]
+                choices.append((max(new), kind, new))
+            _, self.kind[d], load = min(choices)
         self.peers = [d for d in self.order if 0 < sum(v > 0 for v in d) < 3]
+
+    def span_of(self, f, kind):
+        lo, hi = self.base[f], self.base[f] + self.part
+        return (lo + 128 if (f, kind) == (2, 0) else lo, hi - 128 if (f, kind) == (1, 1) else hi)
+
+    def span(self, f, d):
+        return self.span_of(f, self.kind[d])
 
     def along(self, f, values):
         out = [0, 0, 0]
@@ -47,8 +64,8 @@
 
 def kernel(p, ids_ref, cw_ref, go_ref, sg_ref, su_ref, gw_ref, uw_ref, dn_ref, gt_ref, gc_ref,
            xo, s0, s1, s2, r0, r1, r2, g0, g1, g2, gm, ts, tr, gcs, gcr, codes, cws, meta,
-           dna, dnb, gwa, gwb, uwa, uwb, sgt, sut, gbuf, pout, pin, hout, hin,
-           wsem, wss, wsr, s1s, s1r, ds, dr, ps, pr, hs, hr, rs, rr, tss, trs, sas):
+           dna, dnb, gwa, gwb, uwa, uwb, sgt, sut, gbuf, pout, pin, hout, hin, dws, dwr,
+           wsem, wss, wsr, s1s, s1r, ds, dr, ps, pr, hs, hr, rs, rr, tss, trs, sas, es, er, pace):
     n, half, part, planes = p.n, p.half, p.part, p.planes
     send, back, gath = (s0, s1, s2), (r0, r1, r2), (g0, g1, g2)
     me, core = lax.axis_index("expert"), lax.axis_index("etp")
@@ -88,15 +105,26 @@
         first, count = p.tiles[t]
         for j in range(count):
             b = block_of(p.order[first + j])
-            pltpu.make_async_copy(sg_ref.at[b], sgt.at[j], sas.at[0]).start()
-            pltpu.make_async_copy(su_ref.at[b], sut.at[j], sas.at[1]).start()
+            block = pl.ds(pl.multiple_of(b * CAP, CAP), CAP)
+            rows_at = pl.ds(j * CAP, CAP)
+            pltpu.make_async_copy(sg_ref.at[block], sgt.at[rows_at], sas.at[0]).start()
+            pltpu.make_async_copy(su_ref.at[block], sut.at[rows_at], sas.at[1]).start()
 
     def saved_wait(t):
-        count = p.tiles[t][1]
+        count = p.tiles[t][1] * CAP
         pltpu.make_async_copy(sg_ref.at[pl.ds(0, count)], sgt.at[pl.ds(0, count)], sas.at[0]).wait()
         pltpu.make_async_copy(su_ref.at[pl.ds(0, count)], sut.at[pl.ds(0, count)], sas.at[1]).wait()
 
     saved_start(0)
+
+    for f in (1, 2):
+        for a in range(n):
+            for q in range(planes):
+                kind = p.kind[p.along(f, (a, q // n, q % n))]
+                if f == 1 and kind == 1:
+                    back[f][a, q, :, :, part - 128:part] = jnp.zeros((2, CAP, 128), BF16)
+                if f == 2 and kind == 0:
+                    back[f][a, q, :, :, 0:128] = jnp.zeros((2, CAP, 128), BF16)
 
     barrier = pltpu.get_barrier_semaphore()
     for d in p.peers:
@@ -114,14 +142,13 @@
     rows = 2 * planes
     r_iota = lax.broadcasted_iota(I32, (rows, tokens), 0)
 
-    def experts_of(f):
+    def experts_of(f, place, which):
         a, b, c = AXES[f]
-        place = r_iota // 2
         vb = lax.rem(at[b] + place // n, n)
         vc = lax.rem(at[c] + lax.rem(place, n), n)
-        return 2 * (at[a] * stride[a] + vb * stride[b] + vc * stride[c]) + lax.rem(r_iota, 2)
-
-    experts = [experts_of(f).astype(F32) for f in range(3)]
+        return 2 * (at[a] * stride[a] + vb * stride[b] + vc * stride[c]) + which
+
+    experts = [experts_of(f, r_iota // 2, lax.rem(r_iota, 2)).astype(F32) for f in range(3)]
     c_iota = lax.broadcasted_iota(I32, (rows, CAP, tokens), 1).astype(F32)
 
     def select(f, a, info, token_cols):
@@ -138,22 +165,25 @@
         cws[f, a] = weight
         hot = jnp.where(code[:, None, :] == c_iota, 1.0, 0.0)
         hot = hot.reshape(rows * CAP, tokens).astype(BF16)
-        width = p.widths[f]
-        own_slot = p.slot[p.along(f, (a, 0, 0))]
-        for lo in range(0, width, 256):
-            hi = min(lo + 256, width)
+        own_place = p.along(f, (a, 0, 0))
+        own_slot, own_span = p.slot[own_place], p.span(f, own_place)
+        for lo in range(0, part, 256):
+            hi = min(lo + 256, part)
             picked = jnp.dot(hot, token_cols(lo, hi), preferred_element_type=F32).astype(BF16)
             picked = picked.reshape(planes, 2, CAP, hi - lo)
             send[f][a, :, :, :, lo:hi] = picked
-            xo[own_slot, :, :, f * part + lo:f * part + hi] = picked[0]
+            x_lo, x_hi = max(p.base[f] + lo, own_span[0]), min(p.base[f] + hi, own_span[1])
+            if x_lo < x_hi:
+                at_col = x_lo - p.base[f] - lo
+                xo[own_slot, :, :, x_lo:x_hi] = picked[0, :, :, at_col:at_col + x_hi - x_lo]
 
     def dispatch_copy(f, a, q):
         b, c = q // n, q % n
-        width = p.widths[f]
-        slot = p.slot[p.along(f, (a, b, c))]
+        place = p.along(f, (a, b, c))
+        slot, (lo, hi) = p.slot[place], p.span(f, place)
         return pltpu.make_async_remote_copy(
-            src_ref=send[f].at[a, q],
-            dst_ref=xo.at[slot, :, :, pl.ds(f * part, width)],
+            src_ref=send[f].at[a, q, :, :, pl.ds(lo - p.base[f], hi - lo)],
+            dst_ref=xo.at[slot, :, :, pl.ds(lo, hi - lo)],
             send_sem=ds.at[f, p.tile[slot], a],
             recv_sem=dr.at[f, slot],
             device_id=device(p.along(f, (0, b, c))),
@@ -164,7 +194,7 @@
         to = device(p.along(f, (o, 0, 0)))
         return (
             pltpu.make_async_remote_copy(
-                src_ref=go_ref.at[:, pl.ds(f * part, p.widths[f])],
+                src_ref=go_ref.at[:, pl.ds(p.base[f], part)],
                 dst_ref=gath[f].at[o - 1],
                 send_sem=s1s.at[f, o - 1, 0], recv_sem=s1r.at[f, o - 1, 0],
                 device_id=to, device_id_type=MESH),
@@ -182,21 +212,64 @@
         for q in dispatch(f, a, t):
             dispatch_copy(f, a, q).start()
 
+    def bytes_of(spans, sem):
+        lanes = min(256, p.ff)
+        size = sum(hi - lo for lo, hi in spans) * 2 * CAP // lanes
+        rows_at = gwa.at[0, pl.ds(0, size), pl.ds(0, lanes)]
+        return pltpu.make_async_remote_copy(
+            src_ref=rows_at, dst_ref=rows_at, send_sem=sem, recv_sem=sem,
+            device_id=partner, device_id_type=MESH)
+
+    def drain_sent(spans, sem):
+        if spans:
+            bytes_of(spans, sem).wait_send()
+
     def dispatch_sent(f, a, t):
-        k = len(dispatch(f, a, t))
-        if k:
-            pltpu.make_async_remote_copy(
-                src_ref=send[f].at[a, pl.ds(0, k)], dst_ref=send[f].at[a, pl.ds(0, k)],
-                send_sem=ds.at[f, t, a], recv_sem=dr.at[f, 0],
-                device_id=partner, device_id_type=MESH).wait_send()
+        drain_sent([p.span(f, p.along(f, (a, q // n, q % n))) for q in dispatch(f, a, t)], ds.at[f, t, a])
+
+    def group(a):
+        return min(a, n - a)
+
+    def returns(f, t, g):
+        first, count = p.tiles[t]
+        found = [(slot, p.seen(f, p.order[slot])) for slot in range(first, first + count)]
+        return [(slot, d) for slot, d in found if group(d[0]) == g]
 
     def return_copy(f, t, slot):
         a, b, c = p.seen(f, p.order[slot])
+        lo, hi = p.span(f, p.order[slot])
         return pltpu.make_async_remote_copy(
-            src_ref=xo.at[slot, :, :, pl.ds(f * part, part)],
-            dst_ref=back[f].at[a, b * n + c],
-            send_sem=rs.at[f, t], recv_sem=rr.at[f, a],
+            src_ref=xo.at[slot, :, :, pl.ds(lo, hi - lo)],
+            dst_ref=back[f].at[a, b * n + c, :, :, pl.ds(lo - p.base[f], hi - lo)],
+            send_sem=rs.at[f, t, group(a)], recv_sem=rr.at[f, a],
             device_id=device(p.along(f, (0, b, c)), -1), device_id_type=MESH)
+
+    def weight_copy(slot):
+        a, b, c = p.seen(2, p.order[slot])
+        return pltpu.make_async_remote_copy(
+            src_ref=dws.at[slot], dst_ref=dwr.at[a, b * n + c], send_sem=es.at[0], recv_sem=er.at[a],
+            device_id=device(p.along(2, (0, b, c)), -1), device_id_type=MESH)
+
+    def return_start(t, g):
+        lists = [returns(f, t, g) for f in range(3)]
+        for i in range(max(len(v) for v in lists)):
+            for f in range(3):
+                if i < len(lists[f]):
+                    slot, (a, b, c) = lists[f][i]
+                    if (b, c) == (0, 0):
+                        lo, hi = p.span(f, p.order[slot])
+                        back[f][a, 0, :, :, lo - p.base[f]:hi - p.base[f]] = xo[slot, :, :, lo:hi]
+                        if f == 2:
+                            dwr[a, 0] = dws[slot]
+                    else:
+                        if f == 2:
+                            weight_copy(slot).start()
+                        return_copy(f, t, slot).start()
+
+    def return_sent(t, g):
+        for f in range(3):
+            drain_sent([p.span(f, p.order[slot]) for slot, d in returns(f, t, g) if d[1:] != (0, 0)],
+                       rs.at[f, t, g])
 
     last = len(p.tiles) - 1
     pl.semaphore_wait(barrier, len(p.peers) + 1)
@@ -204,10 +277,9 @@
         for f in range(3):
             for copy in gather_copies(f, o):
                 copy.start()
-    for trade in trades:
-        trade.start()
+    trades[0].start()
     for f in range(3):
-        select(f, 0, meta[...], lambda lo, hi: go_ref[:, f * part + lo:f * part + hi])
+        select(f, 0, meta[...], lambda lo, hi: go_ref[:, p.base[f] + lo:p.base[f] + hi])
         dispatch_start(f, 0, 0)
     for a in p.offsets:
         for f in range(3):
@@ -218,9 +290,14 @@
     for a in [0] + p.offsets:
         for f in range(3):
             dispatch_sent(f, a, 0)
-            if last >= 1:
+    pl.semaphore_signal(pace, inc=1, device_id=partner, device_id_type=MESH)
+    pl.semaphore_wait(pace, 1)
+    if last >= 1:
+        for a in [0] + p.offsets:
+            for f in range(3):
                 dispatch_start(f, a, 1)
-
+    for trade in trades[1:]:
+        trade.start()
     for t, (first, count) in enumerate(p.tiles):
         m = count * CAP
         for slot in range(first, first + count):
@@ -254,10 +331,11 @@
             gbuf[l, 0:m, :] = lax.dot_general(features(l), dna[l], NT, preferred_element_type=F32)
             return 0
 
-        def pointwise(l, at_row, j):
+        def pointwise(l, j):
+            at_row = pl.ds(pl.multiple_of(j * CAP, CAP), CAP)
             grad = gbuf[l, at_row, :] + pin[l, at_row, :]
-            gate = sgt[j, l].astype(F32)
-            up = sut[j, l].astype(F32)
+            gate = jnp.swapaxes(sgt[at_row], 0, 1)[l].astype(F32)
+            up = jnp.swapaxes(sut[at_row], 0, 1)[l].astype(F32)
             sig = 0.5 * jnp.tanh(0.5 * gate) + 0.5
             act = gate * sig
             gup = grad * act
@@ -266,25 +344,22 @@
             hout[l, at_row, p.ff:2 * p.ff] = gup.astype(BF16)
             hout[l, at_row, 2 * p.ff:] = jnp.broadcast_to(total, (CAP, 128)).astype(BF16)
 
-        def hidden(l, _):
-            part_copy(l).wait_recv()
-
-            def two(i, _):
-                for k in range(2):
-                    j = 2 * i + k
-                    pointwise(l, pl.ds(pl.multiple_of(j * CAP, CAP), CAP), j)
-                return 0
-
-            lax.fori_loop(0, count // 2, two, 0)
-            if count % 2:
-                pointwise(l, pl.ds((count - 1) * CAP, CAP), count - 1)
-            hidden_copy(l).start()
-            return 0
+        def hidden():
+            for l in range(2):
+                part_copy(l).wait_recv()
+
+                def two(i, _):
+                    pointwise(l, 2 * i)
+                    pointwise(l, 2 * i + 1)
+                    return 0
+
+                lax.fori_loop(0, count // 2, two, 0)
+                if count % 2:
+                    pointwise(l, count - 1)
+                hidden_copy(l).start()
 
         def project(l, _):
             hidden_copy(l).wait_recv()
-            sums = hout[l, 0:m, 2 * p.ff:].astype(F32) + hin[l, 0:m, 2 * p.ff:].astype(F32)
-            xo[pl.ds(first, count), l, :, half:half + 128] = sums.astype(BF16).reshape(count, CAP, 128)
             for lo in range(0, half, p.step):
                 u = None
                 for h, gate_w, up_w in ((hout, gwa, uwa), (hin, gwb, uwb)):
@@ -305,7 +380,7 @@
         lax.fori_loop(0, 2, part_of_other, 0)
         lax.fori_loop(0, 2, part_of_own, 0)
         saved_wait(t)
-        lax.fori_loop(0, 2, hidden, 0)
+        hidden()
         if t < last:
             saved_start(t + 1)
         if t == 0:
@@ -318,21 +393,25 @@
                 for f in range(3):
                     dispatch_start(f, a, t + 2)
         lax.fori_loop(0, 2, project, 0)
+        row = None
+        for l in range(2):
+            sums = hout[l, 0:m, 2 * p.ff:].astype(F32) + hin[l, 0:m, 2 * p.ff:].astype(F32)
+            sums = sums.astype(BF16).astype(F32).reshape(count, CAP, 128)
+            shape = (count, CAP, 128)
+            lane = lax.rem(lax.broadcasted_iota(I32, shape, 2), 2 * CAP)
+            mine = lane == l * CAP + lax.broadcasted_iota(I32, shape, 1)
+            term = jnp.sum(jnp.where(mine, sums, 0.0), axis=1, keepdims=True)
+            row = term if row is None else row + term
+        dws[pl.ds(first, count)] = row
         sent(part_copy)
         sent(hidden_copy)
-        for slot in range(first, first + count):
-            for f in range(3):
-                a, b, c = p.seen(f, p.order[slot])
-                if (b, c) == (0, 0):
-                    back[f][a, 0] = xo[slot, :, :, f * part:(f + 1) * part]
-                else:
-                    return_copy(f, t, slot).start()
+        for g in range(n // 2, 0, -1):
+            return_start(t, g)
 
     def total_copy(f, o):
         to = device(p.along(f, (o, 0, 0)), -1)
-        width = p.widths[f]
         copies = [pltpu.make_async_remote_copy(
-            src_ref=ts.at[f, o - 1, :, pl.ds(0, width)], dst_ref=tr.at[f, o - 1, :, pl.ds(0, width)],
+            src_ref=ts.at[f, o - 1], dst_ref=tr.at[f, o - 1],
             send_sem=tss.at[f, o - 1, 0], recv_sem=trs.at[f, o - 1, 0],
             device_id=to, device_id_type=MESH)]
         if f == 2:
@@ -343,72 +422,94 @@
         return copies
 
     def back_wait(f, a):
-        pltpu.make_async_remote_copy(
-            src_ref=xo.at[pl.ds(0, planes - 1), :, :, pl.ds(0, part)],
-            dst_ref=back[f].at[a, pl.ds(1, planes - 1)],
-            send_sem=rs.at[f, 0], recv_sem=rr.at[f, a],
-            device_id=partner, device_id_type=MESH).wait_recv()
+        spans = [p.span(f, p.along(f, (a, q // n, q % n))) for q in range(1, planes)]
+        bytes_of(spans, rr.at[f, a]).wait_recv()
+        if f == 2:
+            pltpu.make_async_remote_copy(
+                src_ref=dwr.at[a, pl.ds(1, planes - 1)], dst_ref=dwr.at[a, pl.ds(1, planes - 1)],
+                send_sem=es.at[0], recv_sem=er.at[a],
+                device_id=partner, device_id_type=MESH).wait_recv()
 
     def combined(f, a, info):
         back_wait(f, a)
         hit = codes[f, a][:, None, :] == c_iota
         weight = jnp.where(hit, cws[f, a][:, None, :], 0.0)
         weight = weight.reshape(rows * CAP, tokens).astype(BF16)
-        width = p.widths[f]
-        values = back[f][a, :, :, :, 0:width].reshape(rows * CAP, width)
+        values = back[f][a].reshape(rows * CAP, part)
         total = lax.dot_general(weight, values, TN, preferred_element_type=F32)
         if f < 2:
             return total, None
         hot = jnp.where(hit, 1.0, 0.0).reshape(rows * CAP, tokens).astype(BF16)
-        sums = back[f][a, :, :, :, width:part].reshape(rows * CAP, 128)
-        lane = lax.broadcasted_iota(I32, (rows * CAP, 128), 1)
-        row = lax.broadcasted_iota(I32, (rows * CAP, 128), 0) // CAP
-        sums = jnp.where(lane == row, sums.astype(F32), 0.0).astype(BF16)
-        spread = lax.dot_general(sums, hot, TN, preferred_element_type=F32)[0:rows]
+        values = dwr[a].reshape(planes, 128)
+        wide = jnp.concatenate([values] * (rows * CAP // 128), axis=1)
+        wide = jnp.concatenate([wide, wide], axis=0)
+        lane = lax.broadcasted_iota(I32, wide.shape, 1)
+        line = lax.broadcasted_iota(I32, wide.shape, 0)
+        mine = lane // CAP == 2 * lax.rem(line, planes) + line // planes
+        wide = jnp.where(mine, wide, 0.0).astype(BF16)
+        spread = jnp.dot(wide, hot, preferred_element_type=F32)
         info = info.astype(F32)
+        by_choice = experts_of(f, lax.rem(r_iota, planes), r_iota // planes).astype(F32)
         picked = [
-            jnp.sum(jnp.where(experts[f] == info[k:k + 1, :], spread, 0.0), axis=0, keepdims=True)
+            jnp.sum(jnp.where(by_choice == info[k:k + 1, :], spread, 0.0), axis=0, keepdims=True)
             for k in range(p.top)
         ]
         return total, jnp.concatenate(picked, axis=0)
 
-    for a in p.offsets:
+    def partial_sums(a):
         for f in range(3):
             total, sums = combined(f, a, gm[f, a - 1])
-            ts[f, a - 1, :, 0:p.widths[f]] = total.astype(BF16)
+            ts[f, a - 1] = total.astype(BF16)
             if f == 2:
                 gcs[a - 1] = sums
             for copy in total_copy(f, a):
                 copy.start()
+
+    for t in range(last):
+        for g in range(1, n // 2 + 1):
+            return_sent(t, g)
+    if n > 2:
+        return_sent(last, n // 2)
+    return_start(0, 0)
+    for a in p.offsets[::-1]:
+        if group(a) == 1 and a == p.offsets[::-1][0 if n == 2 else 1]:
+            return_sent(last, 1)
+            for t in range(1, last + 1):
+                return_start(t, 0)
+        partial_sums(a)
+    shared = None
     for f in range(3):
         total, sums = combined(f, 0, meta[...])
-        width = p.widths[f]
         for a in range(1, n):
             for copy in total_copy(f, a):
                 copy.wait_recv()
-            total = total + tr[f, a - 1, :, 0:width].astype(F32)
+            total = total + tr[f, a - 1].astype(F32)
             if f == 2:
                 sums = sums + gcr[a - 1]
-        gt_ref[:, f * part:f * part + width] = total.astype(BF16)
+        lo, hi = 0, part
+        if f == 1:
+            shared, hi = total[:, part - 128:], part - 128
         if f == 2:
+            gt_ref[:, p.base[2]:p.base[2] + 128] = (total[:, 0:128] + shared).astype(BF16)
             gc_ref[...] = sums.astype(BF16)
+            lo = 128
+        gt_ref[:, p.base[f] + lo:p.base[f] + hi] = total[:, lo:hi].astype(BF16)
 
     for f in range(3):
-        width = p.widths[f]
         for o in range(1, n):
             for copy in gather_copies(f, o) + tuple(total_copy(f, o)):
                 copy.wait_send()
-        for t, (first, count) in enumerate(p.tiles):
-            if t > 0:
-                for a in range(n):
-                    dispatch_sent(f, a, t)
-            sent = sum(p.seen(f, p.order[s])[1:] != (0, 0) for s in range(first, first + count))
-            if sent:
-                pltpu.make_async_remote_copy(
-                    src_ref=xo.at[pl.ds(0, sent), :, :, pl.ds(0, part)],
-                    dst_ref=xo.at[pl.ds(0, sent), :, :, pl.ds(0, part)],
-                    send_sem=rs.at[f, t], recv_sem=rr.at[f, 0],
-                    device_id=partner, device_id_type=MESH).wait_send()
+        for t in range(1, last + 1):
+            for a in range(n):
+                dispatch_sent(f, a, t)
+    for t in range(last + 1):
+        for g in range(n // 2 + 1):
+            if g == 0:
+                return_sent(t, g)
+    sent_rows = sum(p.seen(2, d)[1:] != (0, 0) for d in p.order)
+    pltpu.make_async_remote_copy(
+        src_ref=dws.at[pl.ds(0, sent_rows)], dst_ref=dws.at[pl.ds(0, sent_rows)],
+        send_sem=es.at[0], recv_sem=er.at[0], device_id=partner, device_id_type=MESH).wait_send()
     for trade in trades:
         trade.wait_send()
 
@@ -418,18 +519,14 @@
     n, half, ff, part, planes = p.n, p.half, p.ff, p.part, p.planes
     tokens, top = expert_ids.shape
     blocks, nt = n * n * n, len(p.tiles)
-    saved = [
-        jnp.transpose(v.reshape(blocks, CAP, 2, ff), (0, 2, 1, 3)) for v in (saved_gate, saved_up)
-    ]
     vmem = pl.BlockSpec(memory_space=pltpu.VMEM)
     hbm = pl.BlockSpec(memory_space=pl.ANY)
     dma = pltpu.SemaphoreType.DMA
     rows = 2 * planes
     scratch = [
-        pltpu.VMEM((blocks, 2, CAP, p.wide), BF16),
-        *[pltpu.VMEM((n, planes, 2, CAP, w), BF16) for w in p.widths],
-        *[pltpu.VMEM((n, planes, 2, CAP, part), BF16) for _ in range(3)],
-        *[pltpu.VMEM((n - 1, tokens, w), BF16) for w in p.widths],
+        pltpu.VMEM((blocks, 2, CAP, half), BF16),
+        *[pltpu.VMEM((n, planes, 2, CAP, part), BF16) for _ in range(6)],
+        *[pltpu.VMEM((n - 1, tokens, part), BF16) for _ in range(3)],
         pltpu.VMEM((3, n - 1, 2 * top, tokens), BF16),
         pltpu.VMEM((3, n - 1, tokens, part), BF16),
         pltpu.VMEM((3, n - 1, tokens, part), BF16),
@@ -441,13 +538,16 @@
         pltpu.VMEM((2, ff, half), BF16),
         pltpu.VMEM((2, ff, half), BF16),
         *[pltpu.VMEM((2, half, ff), BF16) for _ in range(4)],
-        pltpu.VMEM((p.most, 2, CAP, ff), BF16),
-        pltpu.VMEM((p.most, 2, CAP, ff), BF16),
+        pltpu.VMEM((p.most * CAP, 2, ff), BF16),
+        pltpu.VMEM((p.most * CAP, 2, ff), BF16),
         *[pltpu.VMEM((2, p.most * CAP, ff), F32) for _ in range(3)],
         *[pltpu.VMEM((2, p.most * CAP, 2 * ff + 128), BF16) for _ in range(2)],
+        pltpu.VMEM((blocks, 1, 128), F32),
+        pltpu.VMEM((n, planes, 1, 128), F32),
         dma((3,)), dma((3,)), dma((3,)), dma((3, n - 1, 2)), dma((3, n - 1, 2)),
         dma((3, nt, n)), dma((3, blocks)), dma((2,)), dma((2,)), dma((2,)), dma((2,)),
-        dma((3, nt)), dma((3, n)), dma((3, n - 1, 2)), dma((3, n - 1, 2)), dma((2,)),
+        dma((3, nt, n // 2 + 1)), dma((3, n)), dma((3, n - 1, 2)), dma((3, n - 1, 2)), dma((2,)),
+        dma((1,)), dma((n,)), pltpu.SemaphoreType.REGULAR,
     ]
     grad_tokens, grad_combine = pl.pallas_call(
         functools.partial(kernel, p),
@@ -461,7 +561,7 @@
         compiler_params=pltpu.CompilerParams(
             collective_id=0, has_side_effects=True, vmem_limit_bytes=67043328
         ),
-    )(expert_ids.T, combine.T, grad_out, *saved, gate_weight, up_weight, down_weight)
+    )(expert_ids.T, combine.T, grad_out, saved_gate, saved_up, gate_weight, up_weight, down_weight)
     return grad_tokens, grad_combine.T
 
 

time: 159 us -> 143 us (0.90)
  Pallas kernels: 150 us -> 139 us
  local copies, waits for them, and re-layouts: 8.38 us -> 3.07 us
    pallas_call x1, Pallas kernels: 150 us -> 139 us  [on_device(): pl.pallas_call(functools.partial(kernel, p), out_shape=(jax.ShapeDtypeStr...]
    transpose x1 -> x0, local copies, waits for them, and re-layouts: 5.31 us -> none  [on_device(): jnp.transpose(v.reshape(blocks, CAP, 2, ff), (0, 2, 1, 3))]
where the time goes in v3:
time: 143 us; the launch traced here: 142 us
  Pallas kernels  139 us (97%)
  local copies, waits for them, and re-layouts  3.07 us (2%)
    pallas_call x1, Pallas kernels, on_device(): pl.pallas_call(functools.partial(kernel, p), out_shape=(jax.ShapeDtypeStr...  139 us
    unnamed x2, local copies, waits for them, and re-layouts  3.07 us

profile of v3, /device:TPU:1, one launch (start us, length us, event | category | flops | bytes accessed | tf_op | source)
XLA Modules:
  0.0 142.3 jit_solution(12319524315571015229)
XLA Ops:
  0.6 138.6 %shard_map.95 = (bf16[128,1792]{1,0:T(8,128)(2,1)}, bf16[8,128]{1,0:T(8,128)(2,1)}) custom-call(s32[8,128]{1,0:T(8,128)} %bitcast.3, bf16[8,128]{1,0:T(8,128)(2,1)} %bitcast.4, bf16[128,1792]{1,0:T(8,128)(2,1)} %go_ref.1, bf16[1024,2,512]{2,1,0:T(2,128)(2,1)} %sg_ref.1, bf16[1024,2,512]{2,1,0:T(2,128)(2,1)} %su_ref.1, bf16[2,3584,512]{2,1,0:T(8,128)(2,1)} %gw_ref.1, ...), custom_call_target="tpu_custom_call" | custom-call | tf_op jit(solution)/shard_map/pallas_call | solution.py:552
  139.2 1.8 %copy.12 = bf16[128,1792]{1,0:T(8,128)(2,1)} copy(bf16[128,1792]{1,0:T(8,128)(2,1)} %get-tuple-element.8) | data formatting | bytes 917504
  141.1 1.3 copy.13

commit v4 on v3

--- a/solution.py
+++ b/solution.py
@@ -81,6 +81,37 @@
     def block_of(d):
         return device(d, -1)[0]
 
+    for f in (1, 2):
+        for a in range(n):
+            for q in range(planes):
+                kind = p.kind[p.along(f, (a, q // n, q % n))]
+                if f == 1 and kind == 1:
+                    back[f][a, q, :, :, part - 128:part] = jnp.zeros((2, CAP, 128), BF16)
+                if f == 2 and kind == 0:
+                    back[f][a, q, :, :, 0:128] = jnp.zeros((2, CAP, 128), BF16)
+
+    barrier = pltpu.get_barrier_semaphore()
+    for d in p.peers:
+        pl.semaphore_signal(barrier, inc=1, device_id=device(d), device_id_type=MESH)
+    pl.semaphore_signal(barrier, inc=1, device_id=partner, device_id_type=MESH)
+
+    def amount(size, sem):
+        for lanes in (512, 256, 128):
+            rows_in = size // (2 * lanes)
+            if lanes <= p.ff and rows_in * 2 * lanes == size and rows_in % CAP == 0:
+                break
+        rows_at = gwa.at[0, pl.ds(0, rows_in), pl.ds(0, lanes)]
+        return pltpu.make_async_remote_copy(
+            src_ref=rows_at, dst_ref=rows_at, send_sem=sem, recv_sem=sem,
+            device_id=partner, device_id_type=MESH)
+
+    def bytes_of(spans, sem):
+        return amount(sum(hi - lo for lo, hi in spans) * 4 * CAP, sem)
+
+    def drain_sent(spans, sem):
+        if spans:
+            bytes_of(spans, sem).wait_send()
+
     own = pl.multiple_of(core * half, 128)
     other = pl.multiple_of((1 - core) * half, 128)
     loads = [
@@ -116,20 +147,6 @@
         pltpu.make_async_copy(su_ref.at[pl.ds(0, count)], sut.at[pl.ds(0, count)], sas.at[1]).wait()
 
     saved_start(0)
-
-    for f in (1, 2):
-        for a in range(n):
-            for q in range(planes):
-                kind = p.kind[p.along(f, (a, q // n, q % n))]
-                if f == 1 and kind == 1:
-                    back[f][a, q, :, :, part - 128:part] = jnp.zeros((2, CAP, 128), BF16)
-                if f == 2 and kind == 0:
-                    back[f][a, q, :, :, 0:128] = jnp.zeros((2, CAP, 128), BF16)
-
-    barrier = pltpu.get_barrier_semaphore()
-    for d in p.peers:
-        pl.semaphore_signal(barrier, inc=1, device_id=device(d), device_id_type=MESH)
-    pl.semaphore_signal(barrier, inc=1, device_id=partner, device_id_type=MESH)
 
     meta[...] = jnp.concatenate(
         [ids_ref[...].astype(F32), cw_ref[...].astype(F32)], axis=0
@@ -185,10 +202,13 @@
             src_ref=send[f].at[a, q, :, :, pl.ds(lo - p.base[f], hi - lo)],
             dst_ref=xo.at[slot, :, :, pl.ds(lo, hi - lo)],
             send_sem=ds.at[f, p.tile[slot], a],
-            recv_sem=dr.at[f, slot],
+            recv_sem=dr.at[f, p.tile[slot], a],
             device_id=device(p.along(f, (0, b, c))),
             device_id_type=MESH,
         )
+
+    summed = [2 * tokens * part] * 2 + [2 * tokens * part + 4 * p.top * tokens]
+    gathered = 2 * tokens * part + 4 * p.top * tokens
 
     def gather_copies(f, o):
         to = device(p.along(f, (o, 0, 0)))
@@ -196,11 +216,11 @@
             pltpu.make_async_remote_copy(
                 src_ref=go_ref.at[:, pl.ds(p.base[f], part)],
                 dst_ref=gath[f].at[o - 1],
-                send_sem=s1s.at[f, o - 1, 0], recv_sem=s1r.at[f, o - 1, 0],
+                send_sem=s1s.at[f, o - 1], recv_sem=s1r.at[f, o - 1],
                 device_id=to, device_id_type=MESH),
             pltpu.make_async_remote_copy(
                 src_ref=meta, dst_ref=gm.at[f, o - 1],
-                send_sem=s1s.at[f, o - 1, 1], recv_sem=s1r.at[f, o - 1, 1],
+                send_sem=s1s.at[f, o - 1], recv_sem=s1r.at[f, o - 1],
                 device_id=to, device_id_type=MESH),
         )
 
@@ -212,20 +232,11 @@
         for q in dispatch(f, a, t):
             dispatch_copy(f, a, q).start()
 
-    def bytes_of(spans, sem):
-        lanes = min(256, p.ff)
-        size = sum(hi - lo for lo, hi in spans) * 2 * CAP // lanes
-        rows_at = gwa.at[0, pl.ds(0, size), pl.ds(0, lanes)]
-        return pltpu.make_async_remote_copy(
-            src_ref=rows_at, dst_ref=rows_at, send_sem=sem, recv_sem=sem,
-            device_id=partner, device_id_type=MESH)
-
-    def drain_sent(spans, sem):
-        if spans:
-            bytes_of(spans, sem).wait_send()
+    def dispatch_spans(f, a, t):
+        return [p.span(f, p.along(f, (a, q // n, q % n))) for q in dispatch(f, a, t)]
 
     def dispatch_sent(f, a, t):
-        drain_sent([p.span(f, p.along(f, (a, q // n, q % n))) for q in dispatch(f, a, t)], ds.at[f, t, a])
+        drain_sent(dispatch_spans(f, a, t), ds.at[f, t, a])
 
     def group(a):
         return min(a, n - a)
@@ -272,6 +283,8 @@
                        rs.at[f, t, g])
 
     last = len(p.tiles) - 1
+    for f in range(3):
+        select(f, 0, meta[...], lambda lo, hi: go_ref[:, p.base[f] + lo:p.base[f] + hi])
     pl.semaphore_wait(barrier, len(p.peers) + 1)
     for o in p.offsets:
         for f in range(3):
@@ -279,12 +292,10 @@
                 copy.start()
     trades[0].start()
     for f in range(3):
-        select(f, 0, meta[...], lambda lo, hi: go_ref[:, p.base[f] + lo:p.base[f] + hi])
         dispatch_start(f, 0, 0)
     for a in p.offsets:
         for f in range(3):
-            for copy in gather_copies(f, a):
-                copy.wait_recv()
+            amount(gathered, s1r.at[f, a - 1]).wait_recv()
             select(f, a, gm[f, a - 1], lambda lo, hi: gath[f][a - 1, :, lo:hi])
             dispatch_start(f, a, 0)
     for a in [0] + p.offsets:
@@ -300,11 +311,11 @@
         trade.start()
     for t, (first, count) in enumerate(p.tiles):
         m = count * CAP
-        for slot in range(first, first + count):
-            for f in range(3):
-                a, b, c = p.seen(f, p.order[slot])
-                if (b, c) != (0, 0):
-                    dispatch_copy(f, a, b * n + c).wait_recv()
+        for f in range(3):
+            for a in range(n):
+                spans = dispatch_spans(f, a, t)
+                if spans:
+                    bytes_of(spans, dr.at[f, t, a]).wait_recv()
         if t == 0:
             loads[0].wait()
             trades[0].wait_recv()
@@ -412,12 +423,12 @@
         to = device(p.along(f, (o, 0, 0)), -1)
         copies = [pltpu.make_async_remote_copy(
             src_ref=ts.at[f, o - 1], dst_ref=tr.at[f, o - 1],
-            send_sem=tss.at[f, o - 1, 0], recv_sem=trs.at[f, o - 1, 0],
+            send_sem=tss.at[f, o - 1], recv_sem=trs.at[f, o - 1],
             device_id=to, device_id_type=MESH)]
         if f == 2:
             copies.append(pltpu.make_async_remote_copy(
                 src_ref=gcs.at[o - 1], dst_ref=gcr.at[o - 1],
-                send_sem=tss.at[f, o - 1, 1], recv_sem=trs.at[f, o - 1, 1],
+                send_sem=tss.at[f, o - 1], recv_sem=trs.at[f, o - 1],
                 device_id=to, device_id_type=MESH))
         return copies
 
@@ -481,8 +492,7 @@
     for f in range(3):
         total, sums = combined(f, 0, meta[...])
         for a in range(1, n):
-            for copy in total_copy(f, a):
-                copy.wait_recv()
+            amount(summed[f], trs.at[f, a - 1]).wait_recv()
             total = total + tr[f, a - 1].astype(F32)
             if f == 2:
                 sums = sums + gcr[a - 1]
@@ -497,8 +507,8 @@
 
     for f in range(3):
         for o in range(1, n):
-            for copy in gather_copies(f, o) + tuple(total_copy(f, o)):
-                copy.wait_send()
+            amount(gathered, s1s.at[f, o - 1]).wait_send()
+            amount(summed[f], tss.at[f, o - 1]).wait_send()
         for t in range(1, last + 1):
             for a in range(n):
                 dispatch_sent(f, a, t)
@@ -544,9 +554,9 @@
         *[pltpu.VMEM((2, p.most * CAP, 2 * ff + 128), BF16) for _ in range(2)],
         pltpu.VMEM((blocks, 1, 128), F32),
         pltpu.VMEM((n, planes, 1, 128), F32),
-        dma((3,)), dma((3,)), dma((3,)), dma((3, n - 1, 2)), dma((3, n - 1, 2)),
-        dma((3, nt, n)), dma((3, blocks)), dma((2,)), dma((2,)), dma((2,)), dma((2,)),
-        dma((3, nt, n // 2 + 1)), dma((3, n)), dma((3, n - 1, 2)), dma((3, n - 1, 2)), dma((2,)),
+        dma((3,)), dma((3,)), dma((3,)), dma((3, n - 1)), dma((3, n - 1)),
+        dma((3, nt, n)), dma((3, nt, n)), dma((2,)), dma((2,)), dma((2,)), dma((2,)),
+        dma((3, nt, n // 2 + 1)), dma((3, n)), dma((3, n - 1)), dma((3, n - 1)), dma((2,)),
         dma((1,)), dma((n,)), pltpu.SemaphoreType.REGULAR,
     ]
     grad_tokens, grad_combine = pl.pallas_call(

time: 143 us -> 141 us (0.986)
  Pallas kernels: 139 us -> 137 us
    pallas_call x1, Pallas kernels: 139 us -> 137 us  [on_device(): pl.pallas_call(functools.partial(kernel, p), out_shape=(jax.ShapeDtypeStr...]
where the time goes in v4:
time: 141 us; the launch traced here: 140 us
  Pallas kernels  137 us (97%)
  local copies, waits for them, and re-layouts  3.07 us (2%)
    pallas_call x1, Pallas kernels, on_device(): pl.pallas_call(functools.partial(kernel, p), out_shape=(jax.ShapeDtypeStr...  137 us
    unnamed x2, local copies, waits for them, and re-layouts  3.07 us

profile of v4, /device:TPU:1, one launch (start us, length us, event | category | flops | bytes accessed | tf_op | source)
XLA Modules:
  0.0 140.4 jit_solution(2978954562479114576)
XLA Ops:
  0.6 136.7 %shard_map.95 = (bf16[128,1792]{1,0:T(8,128)(2,1)}, bf16[8,128]{1,0:T(8,128)(2,1)}) custom-call(s32[8,128]{1,0:T(8,128)} %bitcast.3, bf16[8,128]{1,0:T(8,128)(2,1)} %bitcast.4, bf16[128,1792]{1,0:T(8,128)(2,1)} %go_ref.1, bf16[1024,2,512]{2,1,0:T(2,128)(2,1)} %sg_ref.1, bf16[1024,2,512]{2,1,0:T(2,128)(2,1)} %su_ref.1, bf16[2,3584,512]{2,1,0:T(8,128)(2,1)} %gw_ref.1, ...), custom_call_target="tpu_custom_call" | custom-call | tf_op jit(solution)/shard_map/pallas_call | solution.py:562
  137.3 1.8 %copy.12 = bf16[128,1792]{1,0:T(8,128)(2,1)} copy(bf16[128,1792]{1,0:T(8,128)(2,1)} %get-tuple-element.8) | data formatting | bytes 917504
  139.2 1.3 copy.13

commit v5 on v4

--- a/solution.py
+++ b/solution.py
@@ -96,11 +96,18 @@
     pl.semaphore_signal(barrier, inc=1, device_id=partner, device_id_type=MESH)
 
     def amount(size, sem):
-        for lanes in (512, 256, 128):
-            rows_in = size // (2 * lanes)
-            if lanes <= p.ff and rows_in * 2 * lanes == size and rows_in % CAP == 0:
-                break
-        rows_at = gwa.at[0, pl.ds(0, rows_in), pl.ds(0, lanes)]
+        units = size // (2 * CAP * 128)
+        found = [
+            (blocks, lines, units // (lines * blocks))
+            for lines in (2, 1) for blocks in range(1, xo.shape[0] + 1)
+            if units % (lines * blocks) == 0 and units // (lines * blocks) <= half // 128
+        ]
+        if found and units * 2 * CAP * 128 == size:
+            blocks, lines, wide = found[0]
+            rows_at = xo.at[pl.ds(0, blocks), pl.ds(0, lines), :, pl.ds(0, 128 * wide)]
+        else:
+            lanes = 256 if size % (512 * CAP) == 0 and p.ff >= 256 else 128
+            rows_at = gwa.at[0, pl.ds(0, size // (2 * lanes)), pl.ds(0, lanes)]
         return pltpu.make_async_remote_copy(
             src_ref=rows_at, dst_ref=rows_at, send_sem=sem, recv_sem=sem,
             device_id=partner, device_id_type=MESH)
@@ -201,8 +208,8 @@
         return pltpu.make_async_remote_copy(
             src_ref=send[f].at[a, q, :, :, pl.ds(lo - p.base[f], hi - lo)],
             dst_ref=xo.at[slot, :, :, pl.ds(lo, hi - lo)],
-            send_sem=ds.at[f, p.tile[slot], a],
-            recv_sem=dr.at[f, p.tile[slot], a],
+            send_sem=ds.at[f, p.tile[slot]],
+            recv_sem=dr.at[f, p.tile[slot]],
             device_id=device(p.along(f, (0, b, c))),
             device_id_type=MESH,
         )
@@ -216,11 +223,11 @@
             pltpu.make_async_remote_copy(
                 src_ref=go_ref.at[:, pl.ds(p.base[f], part)],
                 dst_ref=gath[f].at[o - 1],
-                send_sem=s1s.at[f, o - 1], recv_sem=s1r.at[f, o - 1],
+                send_sem=s1s.at[f], recv_sem=s1r.at[f, o - 1],
                 device_id=to, device_id_type=MESH),
             pltpu.make_async_remote_copy(
                 src_ref=meta, dst_ref=gm.at[f, o - 1],
-                send_sem=s1s.at[f, o - 1], recv_sem=s1r.at[f, o - 1],
+                send_sem=s1s.at[f], recv_sem=s1r.at[f, o - 1],
                 device_id=to, device_id_type=MESH),
         )
 
@@ -235,8 +242,12 @@
     def dispatch_spans(f, a, t):
         return [p.span(f, p.along(f, (a, q // n, q % n))) for q in dispatch(f, a, t)]
 
-    def dispatch_sent(f, a, t):
-        drain_sent(dispatch_spans(f, a, t), ds.at[f, t, a])
+    def tile_spans(f, t):
+        return [span for a in range(n) for span in dispatch_spans(f, a, t)]
+
+    def dispatch_sent(t):
+        for f in range(3):
+            drain_sent(tile_spans(f, t), ds.at[f, t])
 
     def group(a):
         return min(a, n - a)
@@ -252,7 +263,7 @@
         return pltpu.make_async_remote_copy(
             src_ref=xo.at[slot, :, :, pl.ds(lo, hi - lo)],
             dst_ref=back[f].at[a, b * n + c, :, :, pl.ds(lo - p.base[f], hi - lo)],
-            send_sem=rs.at[f, t, group(a)], recv_sem=rr.at[f, a],
+            send_sem=rs.at[f, return_group(t, group(a))], recv_sem=rr.at[f, a],
             device_id=device(p.along(f, (0, b, c)), -1), device_id_type=MESH)
 
     def weight_copy(slot):
@@ -277,10 +288,16 @@
                             weight_copy(slot).start()
                         return_copy(f, t, slot).start()
 
-    def return_sent(t, g):
+    def return_group(t, g):
+        return 3 if g > 0 and t < len(p.tiles) - 1 else g
+
+    def return_sent(which):
         for f in range(3):
-            drain_sent([p.span(f, p.order[slot]) for slot, d in returns(f, t, g) if d[1:] != (0, 0)],
-                       rs.at[f, t, g])
+            drain_sent(
+                [p.span(f, p.order[slot]) for t in range(len(p.tiles)) for g in range(n // 2 + 1)
+                 for slot, d in returns(f, t, g)
+                 if return_group(t, g) == which and d[1:] != (0, 0)],
+                rs.at[f, which])
 
     last = len(p.tiles) - 1
     for f in range(3):
@@ -298,9 +315,7 @@
             amount(gathered, s1r.at[f, a - 1]).wait_recv()
             select(f, a, gm[f, a - 1], lambda lo, hi: gath[f][a - 1, :, lo:hi])
             dispatch_start(f, a, 0)
-    for a in [0] + p.offsets:
-        for f in range(3):
-            dispatch_sent(f, a, 0)
+    dispatch_sent(0)
     pl.semaphore_signal(pace, inc=1, device_id=partner, device_id_type=MESH)
     pl.semaphore_wait(pace, 1)
     if last >= 1:
@@ -312,10 +327,8 @@
     for t, (first, count) in enumerate(p.tiles):
         m = count * CAP
         for f in range(3):
-            for a in range(n):
-                spans = dispatch_spans(f, a, t)
-                if spans:
-                    bytes_of(spans, dr.at[f, t, a]).wait_recv()
+            if tile_spans(f, t):
+                bytes_of(tile_spans(f, t), dr.at[f, t]).wait_recv()
         if t == 0:
             loads[0].wait()
             trades[0].wait_recv()
@@ -423,12 +436,12 @@
         to = device(p.along(f, (o, 0, 0)), -1)
         copies = [pltpu.make_async_remote_copy(
             src_ref=ts.at[f, o - 1], dst_ref=tr.at[f, o - 1],
-            send_sem=tss.at[f, o - 1], recv_sem=trs.at[f, o - 1],
+            send_sem=tss.at[f], recv_sem=trs.at[f],
             device_id=to, device_id_type=MESH)]
         if f == 2:
             copies.append(pltpu.make_async_remote_copy(
                 src_ref=gcs.at[o - 1], dst_ref=gcr.at[o - 1],
-                send_sem=tss.at[f, o - 1], recv_sem=trs.at[f, o - 1],
+                send_sem=tss.at[f], recv_sem=trs.at[f],
                 device_id=to, device_id_type=MESH))
         return copies
 
@@ -476,23 +489,21 @@
             for copy in total_copy(f, a):
                 copy.start()
 
-    for t in range(last):
-        for g in range(1, n // 2 + 1):
-            return_sent(t, g)
+    return_sent(3)
     if n > 2:
-        return_sent(last, n // 2)
+        return_sent(2)
     return_start(0, 0)
     for a in p.offsets[::-1]:
         if group(a) == 1 and a == p.offsets[::-1][0 if n == 2 else 1]:
-            return_sent(last, 1)
+            return_sent(1)
             for t in range(1, last + 1):
                 return_start(t, 0)
         partial_sums(a)
     shared = None
     for f in range(3):
         total, sums = combined(f, 0, meta[...])
+        amount((n - 1) * summed[f], trs.at[f]).wait_recv()
         for a in range(1, n):
-            amount(summed[f], trs.at[f, a - 1]).wait_recv()
             total = total + tr[f, a - 1].astype(F32)
             if f == 2:
                 sums = sums + gcr[a - 1]
@@ -506,16 +517,11 @@
         gt_ref[:, p.base[f] + lo:p.base[f] + hi] = total[:, lo:hi].astype(BF16)
 
     for f in range(3):
-        for o in range(1, n):
-            amount(gathered, s1s.at[f, o - 1]).wait_send()
-            amount(summed[f], tss.at[f, o - 1]).wait_send()
-        for t in range(1, last + 1):
-            for a in range(n):
-                dispatch_sent(f, a, t)
-    for t in range(last + 1):
-        for g in range(n // 2 + 1):
-            if g == 0:
-                return_sent(t, g)
+        amount((n - 1) * gathered, s1s.at[f]).wait_send()
+        amount((n - 1) * summed[f], tss.at[f]).wait_send()
+    for t in range(1, last + 1):
+        dispatch_sent(t)
+    return_sent(0)
     sent_rows = sum(p.seen(2, d)[1:] != (0, 0) for d in p.order)
     pltpu.make_async_remote_copy(
         src_ref=dws.at[pl.ds(0, sent_rows)], dst_ref=dws.at[pl.ds(0, sent_rows)],
@@ -554,9 +560,9 @@
         *[pltpu.VMEM((2, p.most * CAP, 2 * ff + 128), BF16) for _ in range(2)],
         pltpu.VMEM((blocks, 1, 128), F32),
         pltpu.VMEM((n, planes, 1, 128), F32),
-        dma((3,)), dma((3,)), dma((3,)), dma((3, n - 1)), dma((3, n - 1)),
-        dma((3, nt, n)), dma((3, nt, n)), dma((2,)), dma((2,)), dma((2,)), dma((2,)),
-        dma((3, nt, n // 2 + 1)), dma((3, n)), dma((3, n - 1)), dma((3, n - 1)), dma((2,)),
+        dma((3,)), dma((3,)), dma((3,)), dma((3,)), dma((3, n - 1)),
+        dma((3, nt)), dma((3, nt)), dma((2,)), dma((2,)), dma((2,)), dma((2,)),
+        dma((3, 4)), dma((3, n)), dma((3,)), dma((3,)), dma((2,)),
         dma((1,)), dma((n,)), pltpu.SemaphoreType.REGULAR,
     ]
     grad_tokens, grad_combine = pl.pallas_call(

time: 141 us -> 140 us (level)
  no operation moved by 1% of the time
where the time goes in v5:
time: 140 us
  Pallas kernels  136 us (97%)
  local copies, waits for them, and re-layouts  3.07 us (2%)
    pallas_call x1, Pallas kernels, on_device(): pl.pallas_call(functools.partial(kernel, p), out_shape=(jax.ShapeDtypeStr...  136 us
    unnamed x2, local copies, waits for them, and re-layouts  3.07 us

profile of v5, /device:TPU:1, one launch (start us, length us, event | category | flops | bytes accessed | tf_op | source)
XLA Modules:
  0.0 139.8 jit_solution(16142664619243147841)
XLA Ops:
  0.6 136.1 %shard_map.95 = (bf16[128,1792]{1,0:T(8,128)(2,1)}, bf16[8,128]{1,0:T(8,128)(2,1)}) custom-call(s32[8,128]{1,0:T(8,128)} %bitcast.3, bf16[8,128]{1,0:T(8,128)(2,1)} %bitcast.4, bf16[128,1792]{1,0:T(8,128)(2,1)} %go_ref.1, bf16[1024,2,512]{2,1,0:T(2,128)(2,1)} %sg_ref.1, bf16[1024,2,512]{2,1,0:T(2,128)(2,1)} %su_ref.1, bf16[2,3584,512]{2,1,0:T(8,128)(2,1)} %gw_ref.1, ...), custom_call_target="tpu_custom_call" | custom-call | tf_op jit(solution)/shard_map/pallas_call | solution.py:568
  136.7 1.8 %copy.12 = bf16[128,1792]{1,0:T(8,128)(2,1)} copy(bf16[128,1792]{1,0:T(8,128)(2,1)} %get-tuple-element.8) | data formatting | bytes 917504
  138.5 1.3 copy.13
